TPU v7x, 256 devices: a whole 4x4x8 slice. The times are simulated.
256 devices in a mesh: dp: 32 (over y, x, z_lo), mp: 8 (over z_hi, core).
Axes of the slice: x: 4, y: 4, z: 8 (z_hi: 4, z_lo: 2; z = z_hi * 2 + z_lo), core: 2. Of those that a mesh axis runs over, the one named last changes fastest.
Arguments:
- hidden: bfloat16 [65536, 13824], P('dp', 'mp'), may hold values from -6 to 6
- out_grad: bfloat16 [65536, 5120], P('dp', 'mp'), may hold values from -6 to 6
- proj_in: bfloat16 [64, 13824], P(None, 'mp'), may hold values from -0.0546875 to 0.0546875
- proj_out: bfloat16 [64, 5120], P(None, 'mp'), may hold values from -0.078125 to 0.078125
- segment_ids: int32 [32, 2048], P('dp'), may hold values from 0 to 15, never falling along the last dimension, each value on 1 to 1024 neighbouring positions
Outputs:
- features: float32 [512, 4096], P('dp')
- gram: float32 [4096, 4096], P(('dp', 'mp'))
Inputs may be any that keep to these rules, and one draw needn't show every extreme that they name: `segment_ids`: within each row the numbers never fall; each of the 16 numbers names 1 to 1024 tokens of the row.
All inputs are finite; a program needn't handle non-finite values.
Results may differ from a plain program's by a relative error of at most 0.0003.
Values sent between devices are 32-bit elements; how exact they have to be, the bound alone decides.
A program may use at most 64 MiB of HBM per device.

v0:
```python
import jax
import jax.numpy as jnp
from jax import lax
from jax.sharding import PartitionSpec as P

EX_DEV = 16


def in_blocks(array, dim, length):
    before, after = (array.shape[:dim], array.shape[dim + 1 :])
    return jnp.moveaxis(array.reshape(*before, length, -1, *after), dim, 0)


def sent_and_summed(array, axis, dim):
    tiles = in_blocks(array, dim, lax.axis_size(axis))
    arrived = lax.all_to_all(tiles, axis, split_axis=0, concat_axis=0, tiled=True)
    return arrived.sum(axis=0)


def copy_for_each(array, axis):
    length = lax.axis_size(axis)
    return lax.all_to_all(
        jnp.broadcast_to(array[None], (length, *array.shape)), axis, 0, 0, tiled=True
    )


def over_copies(array, axis):
    return copy_for_each(array, axis).sum(axis=0)


def in_order(tiles, dim):
    shape = list(tiles.shape[1:])
    shape[dim] *= tiles.shape[0]
    return jnp.moveaxis(tiles, 0, dim).reshape(shape)


def collect(array, axis, dim):
    return in_order(copy_for_each(array, axis), dim)


def outer_sums(onehot, projected, width):
    inputs = projected[:, :width]
    outputs = projected[:, width:]
    weighted = onehot[:, :, None] * outputs[None, :, :]
    grads = jnp.einsum("eti,tj->eij", weighted, inputs, precision=lax.Precision.HIGHEST)
    return grads.reshape(onehot.shape[0], width * width)


def body(hidden, out_grad, proj_in, proj_out, segment_ids):
    width = proj_in.shape[0]
    examples = EX_DEV
    inputs = lax.dot_general(
        hidden, proj_in, (((1,), (1,)), ((), ())), preferred_element_type=jnp.float32
    )
    outputs = lax.dot_general(
        out_grad, proj_out, (((1,), (1,)), ((), ())), preferred_element_type=jnp.float32
    )
    projected = jnp.concatenate([inputs, outputs], axis=1)
    example_ids = segment_ids[0]
    onehot = (example_ids[None, :] == jnp.arange(examples, dtype=jnp.int32)[:, None]).astype(
        jnp.float32
    )
    counts = jnp.sum(onehot, axis=1)
    portion = sent_and_summed(projected, "mp", 0)
    tokens_each = portion.shape[0]
    own_onehot = lax.dynamic_slice_in_dim(
        onehot, lax.axis_index("mp") * tokens_each, tokens_each, 1
    )
    grads = over_copies(outer_sums(own_onehot, portion, width), "mp")
    features = grads / jnp.sqrt(counts)[:, None]
    proj_size = width * width
    data_count = lax.axis_size("dp")
    model_count = lax.axis_size("mp")
    total_examples = examples * data_count
    share = proj_size // model_count
    own_cols = lax.dynamic_slice_in_dim(features, lax.axis_index("mp") * share, share, 1)
    all_cols = collect(own_cols, "dp", 0)
    all_rows = lax.all_to_all(features, "dp", split_axis=1, concat_axis=0, tiled=True)
    block = lax.dot_general(
        all_rows,
        all_cols,
        (((0,), (0,)), ((), ())),
        precision=lax.Precision.HIGHEST,
        preferred_element_type=jnp.float32,
    )
    gram_rows = lax.all_to_all(block, "mp", split_axis=0, concat_axis=1, tiled=True)
    return (features, gram_rows / total_examples)


def solution(mesh):
    placed = (P("dp", "mp"), P("dp", "mp"), P(None, "mp"), P(None, "mp"), P("dp", None))
    return jax.shard_map(
        body,
        mesh=mesh,
        in_specs=placed,
        out_specs=(P("dp", None), P(("dp", "mp"), None)),
        check_vma=False,
    )
```

profile of v0, /device:TPU:1, one launch (start us, length us, event | category | flops | bytes accessed | tf_op | source)
XLA Modules:
  0.0 166.9 jit_solution(10002467775457512897)
XLA Ops:
  0.6 0.0 copy-start
  0.6 0.0 copy-start.2
  0.7 1.7 %copy-done = bf16[2048,640]{1,0:T(8,128)(2,1)S(1)} copy-done((bf16[2048,640]{1,0:T(8,128)(2,1)S(1)}, bf16[2048,640]{1,0:T(8,128)(2,1)}, u32[]{:S(2)}) %copy-start) | copy-done | bytes 2621464
  2.4 1.8 %fusion.6 = f32[2048,64]{0,1:T(8,128)S(1)} fusion(bf16[2048,640]{1,0:T(8,128)(2,1)S(1)} %copy-done, bf16[64,640]{1,0:T(8,128)(2,1)} %param.8), kind=kOutput, calls=%fused_computation.15 | convolution fusion | flops 167772160 | bytes 3227648 | tf_op jit(solution)/shard_map/dot_general | solution.py:55
  4.2 0.0 copy-done.2
  4.2 4.4 %fusion.8 = f32[2048,64]{0,1:T(8,128)S(1)} fusion(bf16[64,1728]{1,0:T(8,128)(2,1)S(1)} %copy-done.2, bf16[2048,1728]{0,1:T(8,128)(2,1)} %param.5), kind=kOutput, calls=%fused_computation.17 | convolution fusion | flops 452984832 | bytes 7823360 | tf_op jit(solution)/shard_map/dot_general | solution.py:52
  8.6 0.1 pad_maximum_fusion
  8.7 0.0 copy-start.3
  8.7 1.1 copy.25
  9.8 10.0 %all-to-all-start = ((f32[8,256,128]{1,2,0:T(8,128)}), f32[8,256,128]{1,2,0:T(8,128)}, u32[]{:S(2)}, u32[]{:S(2)}) async-start(f32[8,256,128]{1,2,0:T(8,128)} %bitcast.30), calls=%async_computation | async-start | bytes 2097152 | tf_op jit(solution)/shard_map/all_to_all | solution.py:16
  19.8 0.0 copy-done.3
  19.8 24.0 %all-to-all-done = f32[8,256,128]{1,2,0:T(8,128)} async-done(((f32[8,256,128]{1,2,0:T(8,128)}), f32[8,256,128]{1,2,0:T(8,128)}, u32[]{:S(2)}, u32[]{:S(2)}) %all-to-all-start) | async-done | bytes 1048608 | tf_op jit(solution)/shard_map/all_to_all | solution.py:16
  43.8 1.3 reduce_sum.29
  45.2 1.0 fusion
  46.1 0.2 broadcast_in_dim.6
  46.3 1.5 broadcast_in_dim.7
  47.8 9.5 %all-to-all-start.1 = ((f32[8,16,4096]{2,1,0:T(8,128)}), f32[8,16,4096]{2,1,0:T(8,128)}, u32[]{:S(2)}, u32[]{:S(2)}) async-start(f32[8,16,4096]{2,1,0:T(8,128)} %broadcast_in_dim.7), calls=%async_computation.1 | async-start | bytes 4194304 | tf_op jit(solution)/shard_map/all_to_all | solution.py:22
  57.3 0.1 fusion.5
  57.5 44.8 %all-to-all-done.1 = f32[8,16,4096]{2,1,0:T(8,128)} async-done(((f32[8,16,4096]{2,1,0:T(8,128)}), f32[8,16,4096]{2,1,0:T(8,128)}, u32[]{:S(2)}, u32[]{:S(2)}) %all-to-all-start.1) | async-done | bytes 2097184 | tf_op jit(solution)/shard_map/all_to_all | solution.py:22
  102.3 1.7 %reduce_sum.30 = f32[16,4096]{1,0:T(8,128)S(1)} reduce(f32[8,16,4096]{2,1,0:T(8,128)} %all-to-all-done.1, f32[]{:T(128)} %constant.5.clone.1), dimensions={0}, to_apply=%region_1.0 | reduce | flops 458752 | bytes 2359300 | tf_op jit(solution)/shard_map/reduce_sum | solution.py:28
  104.0 0.1 copy.23
  104.1 0.1 bitcast_divide_fusion
  104.1 0.9 copy.18
  105.0 13.4 %all-to-all-start.2 = ((f32[16,32,128]{2,0,1:T(8,128)}), f32[16,32,128]{2,0,1:T(8,128)S(1)}, u32[]{:S(2)}, u32[]{:S(2)}) async-start(f32[16,32,128]{2,0,1:T(8,128)} %copy.18), calls=%async_computation.2 | async-start | bytes 524288 | tf_op jit(solution)/shard_map/all_to_all | solution.py:78
  118.4 0.1 broadcast_divide_fusion
  118.5 0.0 copy-start.1
  118.5 8.3 %all-to-all-done.2 = f32[16,32,128]{2,0,1:T(8,128)S(1)} async-done(((f32[16,32,128]{2,0,1:T(8,128)}), f32[16,32,128]{2,0,1:T(8,128)S(1)}, u32[]{:S(2)}, u32[]{:S(2)}) %all-to-all-start.2) | async-done | bytes 262176 | tf_op jit(solution)/shard_map/all_to_all | solution.py:78
  126.8 1.1 broadcast_in_dim.8
  128.0 4.7 %all-to-all-start.3 = ((f32[32,16,512]{2,1,0:T(8,128)}), f32[32,16,512]{2,1,0:T(8,128)}, u32[]{:S(2)}, u32[]{:S(2)}) async-start(f32[32,16,512]{2,1,0:T(8,128)} %broadcast_in_dim.8), calls=%async_computation.3 | async-start | bytes 2097152 | tf_op jit(solution)/shard_map/all_to_all | solution.py:22
  132.6 0.1 copy.19
  132.8 15.5 %all-to-all-done.3 = f32[32,16,512]{2,1,0:T(8,128)} async-done(((f32[32,16,512]{2,1,0:T(8,128)}), f32[32,16,512]{2,1,0:T(8,128)}, u32[]{:S(2)}, u32[]{:S(2)}) %all-to-all-start.3) | async-done | bytes 1048608 | tf_op jit(solution)/shard_map/all_to_all | solution.py:22
  148.2 1.9 %fusion.7 = f32[8,16,512]{2,1,0:T(8,128)S(1)} fusion(f32[8,16,512]{2,1,0:T(8,128)S(1)} %bitcast.34, f32[512,512,1]{1,0,2:T(8,128)} %bitcast.7), kind=kOutput, calls=%fused_computation.16 | convolution fusion | flops 402653184 | bytes 1572864 | tf_op jit(solution)/shard_map/dot_general | solution.py:79
  150.2 0.0 copy-done.1
  150.2 15.9 %all_to_all.41 = f32[8,16,512]{2,1,0:T(8,128)S(1)} all-to-all(f32[8,16,512]{2,1,0:T(8,128)S(1)} %fusion.7), channel_id=1, replica_groups=mesh['dp'=32,'mp'=8] {'mp'}, dimensions={0} | all-to-all | bytes 524288 | tf_op jit(solution)/shard_map/all_to_all | solution.py:86
  166.2 0.7 copy.22
  (6 shorter events, 0.1 us)
Async XLA Ops:
  0.6 1.7 %copy-start = (bf16[2048,640]{1,0:T(8,128)(2,1)S(1)}, bf16[2048,640]{1,0:T(8,128)(2,1)}, u32[]{:S(2)}) copy-start(bf16[2048,640]{1,0:T(8,128)(2,1)} %param.6) | copy-start | bytes 7864324
  0.6 3.5 %copy-start.2 = (bf16[64,1728]{1,0:T(8,128)(2,1)S(1)}, bf16[64,1728]{1,0:T(8,128)(2,1)}, u32[]{:S(2)}) copy-start(bf16[64,1728]{1,0:T(8,128)(2,1)} %param.7) | copy-start | bytes 663556
  8.7 11.1 %copy-start.3 = (s32[1,2048]{1,0:T(1,128)S(1)}, s32[1,2048]{1,0:T(1,128)}, u32[]{:S(2)}) copy-start(s32[1,2048]{1,0:T(1,128)} %param.9) | copy-start | bytes 24580
  9.8 34.0 %all-to-all-start = ((f32[8,256,128]{1,2,0:T(8,128)}), f32[8,256,128]{1,2,0:T(8,128)}, u32[]{:S(2)}, u32[]{:S(2)}) async-start(f32[8,256,128]{1,2,0:T(8,128)} %bitcast.30), calls=%async_computation | async-start | bytes 2097152 | tf_op jit(solution)/shard_map/all_to_all | solution.py:16
  47.8 54.4 %all-to-all-start.1 = ((f32[8,16,4096]{2,1,0:T(8,128)}), f32[8,16,4096]{2,1,0:T(8,128)}, u32[]{:S(2)}, u32[]{:S(2)}) async-start(f32[8,16,4096]{2,1,0:T(8,128)} %broadcast_in_dim.7), calls=%async_computation.1 | async-start | bytes 4194304 | tf_op jit(solution)/shard_map/all_to_all | solution.py:22
  105.0 21.8 %all-to-all-start.2 = ((f32[16,32,128]{2,0,1:T(8,128)}), f32[16,32,128]{2,0,1:T(8,128)S(1)}, u32[]{:S(2)}, u32[]{:S(2)}) async-start(f32[16,32,128]{2,0,1:T(8,128)} %copy.18), calls=%async_computation.2 | async-start | bytes 524288 | tf_op jit(solution)/shard_map/all_to_all | solution.py:78
  118.5 31.7 %copy-start.1 = (f32[16,4096]{1,0:T(8,128)}, f32[16,4096]{1,0:T(8,128)S(1)}, u32[]{:S(2)}) copy-start(f32[16,4096]{1,0:T(8,128)S(1)} %broadcast_divide_fusion) | copy-start | bytes 786436
  128.0 20.3 %all-to-all-start.3 = ((f32[32,16,512]{2,1,0:T(8,128)}), f32[32,16,512]{2,1,0:T(8,128)}, u32[]{:S(2)}, u32[]{:S(2)}) async-start(f32[32,16,512]{2,1,0:T(8,128)} %broadcast_in_dim.8), calls=%async_computation.3 | async-start | bytes 2097152 | tf_op jit(solution)/shard_map/all_to_all | solution.py:22
where the time goes:
time: 168 us; the launch traced here: 167 us
  waiting for transfers between devices  92.6 us (55%)
  starting transfers between devices  37.4 us (22%)
  blocking collectives  15.9 us (9%)
  matrix products  9.1 us (5%)
  local copies, waits for them, and re-layouts  7.5 us (4%)
  other arithmetic  3.43 us (2%)
    all_to_all x2, waiting for transfers between devices, copy_for_each(): lax.all_to_all(jnp.broadcast_to(array[None], (length, *array.shape)), axi...  60.3 us
    all_to_all x1, waiting for transfers between devices, sent_and_summed(): lax.all_to_all(tiles, axis, split_axis=0, concat_axis=0, tiled=True)  24 us
    all_to_all x1, blocking collectives, body(): lax.all_to_all(block, 'mp', split_axis=0, concat_axis=1, tiled=True)  15.9 us
    all_to_all x2, starting transfers between devices, copy_for_each(): lax.all_to_all(jnp.broadcast_to(array[None], (length, *array.shape)), axi...  14.1 us
    all_to_all x1, starting transfers between devices, body(): lax.all_to_all(features, 'dp', split_axis=1, concat_axis=0, tiled=True)  13.4 us
    all_to_all x1, starting transfers between devices, sent_and_summed(): lax.all_to_all(tiles, axis, split_axis=0, concat_axis=0, tiled=True)  9.96 us
    all_to_all x1, waiting for transfers between devices, body(): lax.all_to_all(features, 'dp', split_axis=1, concat_axis=0, tiled=True)  8.3 us
    dot_general x1, matrix products, body(): lax.dot_general(hidden, proj_in, (((1,), (1,)), ((), ())), preferred_elem...  4.4 us
  transfers between devices with their start and end apart: 4, of which 4 were waited for; matrix products, arithmetic and copies ran while one was open for 0% of the time, Pallas kernels for 0%

commit v1 on v0

v1 whole, which is shorter than its diff:
```python
import jax
import jax.numpy as jnp
from jax import lax
from jax.experimental import pallas as pl
from jax.experimental.pallas import tpu as pltpu
from jax.sharding import PartitionSpec as P

MESH = pl.DeviceIdType.MESH
EX = 16
DP = 32
MP = 8
F32 = jnp.float32
BF16 = jnp.bfloat16


def split(x):
    hi = x.astype(BF16)
    return hi, (x - hi.astype(F32)).astype(BF16)


def dot_nt(a, b):
    return lax.dot_general(a, b, (((1,), (1,)), ((), ())), preferred_element_type=F32)


def dot(a, b):
    return lax.dot_general(a, b, (((1,), (0,)), ((), ())), preferred_element_type=F32)


def kernel(
    hid,
    og,
    pin,
    pout,
    seg,
    feat_o,
    gram_o,
    hbuf,
    gbuf,
    wh,
    wg,
    psend,
    pmine,
    precv,
    zrecv,
    zrel,
    pown,
    ppart,
    whi,
    wlo,
    rb,
    gbuf2,
    brecv,
    fown,
    fpar,
    fparp,
    cc,
    rr,
    rrp,
    gb,
    gg,
    lsem,
    d2d_s,
    d2d_r,
    z_s,
    z_r,
    px_s,
    px_r,
    b_s,
    b_r,
    c1_s,
    c1_r,
    c2_s,
    c2_r,
    c3_s,
    c3_r,
    c4_s,
    c4_r,
    ft_s,
    ft_r,
    dd_s,
    dd_r,
):
    dp = lax.axis_index("dp")
    m = lax.axis_index("mp")
    c = m // 2
    h = m % 2
    p = dp // 2
    zl = dp % 2
    partner = c * 2 + (1 - h)
    nblk = 256

    def rc(src, dst, ss, rs, tdp, tmp):
        return pltpu.make_async_remote_copy(
            src_ref=src,
            dst_ref=dst,
            send_sem=ss,
            recv_sem=rs,
            device_id=(tdp, tmp),
            device_id_type=MESH,
        )

    owners = [(c + 2) % 4, (c + 1) % 4, (c + 3) % 4, c]
    blocks = []
    for o in owners:
        blocks.append(o * 2 + (1 - h))
        blocks.append(o * 2 + h)
    loads = []
    for k, blk in enumerate(blocks):
        rows = pl.ds(pl.multiple_of(blk * nblk, nblk), nblk)
        a = pltpu.make_async_copy(hid.at[rows], hbuf.at[k], lsem.at[2 * k])
        b = pltpu.make_async_copy(og.at[rows], gbuf.at[k], lsem.at[2 * k + 1])
        a.start()
        b.start()
        loads.append((a, b))

    barrier = pltpu.get_barrier_semaphore()

    def greet_dp(k, carry):
        pl.semaphore_signal(barrier, inc=1, device_id=((dp + k) % DP, m), device_id_type=MESH)
        return carry

    lax.fori_loop(1, DP, greet_dp, 0)

    def greet_own(k, carry):
        pl.semaphore_signal(barrier, inc=1, device_id=(dp, (m + k) % MP), device_id_type=MESH)
        pl.semaphore_signal(
            barrier, inc=1, device_id=(2 * p + (1 - zl), (m + k) % MP), device_id_type=MESH
        )
        return carry

    lax.fori_loop(1, MP, greet_own, 0)

    wh[0:64, :] = pin[...]
    wh[64:128, :] = jnp.zeros((64, wh.shape[1]), BF16)
    wg[0:64, :] = jnp.zeros((64, wg.shape[1]), BF16)
    wg[64:128, :] = pout[...]

    segv = seg[...]
    erow = lax.broadcasted_iota(jnp.int32, (EX, segv.shape[1]), 0)
    counts = jnp.sum(jnp.where(erow == segv, 1.0, 0.0).astype(F32), axis=1, keepdims=True)
    scale = 1.0 / jnp.sqrt(counts)

    def project(k):
        loads[k][0].wait()
        loads[k][1].wait()
        return dot_nt(hbuf[k], wh[...]) + dot_nt(gbuf[k], wg[...])

    d2d = []
    zsend = []
    up = (c + 1) % 4
    down = (c + 3) % 4

    def zcopy(k, src, to):
        return rc(src, zrecv.at[k], z_s.at[k], z_r.at[k], dp, to * 2 + h)

    def finish(k):
        d2d[k].wait_recv()
        pmine[k] = pmine[k] + precv[k]
        if k == 0:
            zsend.append(zcopy(0, pmine.at[0, 0:128], down))
            zsend.append(zcopy(1, pmine.at[0, 128:256], up))
            zsend[0].start()
            zsend[1].start()
        if k == 1:
            zsend.append(zcopy(2, pmine.at[1, 0:128], up))
            zsend[2].start()
        if k == 2:
            zsend.append(zcopy(3, pmine.at[2, 128:256], down))
            zsend[3].start()

    for k in range(4):
        psend[k] = project(2 * k)
        if k == 0:
            pl.semaphore_wait(barrier, DP - 1 + 2 * (MP - 1))
        d2d.append(rc(psend.at[k], precv.at[k], d2d_s.at[k], d2d_r.at[k], dp, partner))
        d2d[k].start()
        pmine[k] = project(2 * k + 1)
        if k >= 1:
            finish(k - 1)
    finish(3)

    zsend[0].wait_recv()
    zrel[0] = zrecv[0] + pmine[2, 0:128]
    zsend.append(zcopy(4, zrel.at[0], down))
    zsend[4].start()
    zsend[1].wait_recv()
    zrel[1] = zrecv[1] + pmine[1, 128:256]
    zsend.append(zcopy(5, zrel.at[1], up))
    zsend[5].start()
    zsend[2].wait_recv()
    zsend[3].wait_recv()
    zsend[4].wait_recv()
    zsend[5].wait_recv()
    pown[0:128] = pmine[3, 0:128] + zrecv[2] + zrecv[4]
    pown[128:256] = pmine[3, 128:256] + zrecv[3] + zrecv[5]

    px = rc(pown, ppart, px_s, px_r, dp, partner)
    px.start()

    def weigh(s, toks, blk):
        low = jnp.where(lax.broadcasted_iota(jnp.int32, (nblk, 128), 1) < 64, toks, 0.0)
        high = pltpu.roll(low, 64, 1)
        lh, ll = split(low)
        hh, hl = split(high)
        base = s * 512
        rb[base : base + 256, 0:128] = lh
        rb[base : base + 256, 128:256] = ll
        rb[base + 256 : base + 512, 0:128] = hh
        rb[base + 256 : base + 512, 128:256] = hl
        trans = toks.T
        ids = seg[:, pl.ds(pl.multiple_of(blk * nblk, nblk), nblk)]
        mask = lax.broadcasted_iota(jnp.int32, (EX, nblk), 0) == ids
        for cq in range(4):
            rows = jnp.where(h == 0, trans[64 + 16 * cq : 72 + 16 * cq], trans[72 + 16 * cq : 80 + 16 * cq])
            for k in range(4):
                tile = (cq * 2 + k % 2) * 2 + k // 2
                for par in range(2):
                    one = jnp.where(mask, rows[2 * k + par : 2 * k + par + 1, :], 0.0)
                    oh, ol = split(one)
                    whi[tile * 16 : tile * 16 + 16, base + par * 256 : base + par * 256 + 256] = oh
                    wlo[tile * 16 : tile * 16 + 16, base + par * 256 : base + par * 256 + 256] = ol

    def grads(s):
        cols = slice(s * 512, s * 512 + 512)
        both = dot(whi[:, cols], rb[cols, :])
        return both[:, 0:128] + both[:, 128:256] + dot(wlo[:, cols], rb[cols, 0:128])

    weigh(0, pown[...], m)
    g0 = grads(0)
    px.wait_recv()
    weigh(1, ppart[...], partner)
    gbuf2[...] = (g0 + grads(1)).reshape(4, 2, 2, 16, 128)

    bs = []
    for k in (2, 1, 3):
        to = (c + k) % 4
        cp = rc(gbuf2.at[to], brecv.at[k - 1], b_s.at[k - 1], b_r.at[k - 1], dp, to * 2 + h)
        cp.start()
        bs.append(cp)
    for cp in bs:
        cp.wait_recv()
    fown[...] = (gbuf2[c] + brecv[0] + brecv[1] + brecv[2]) * scale[None, None]

    def c2(k):
        to = (m + k) % MP
        return rc(fown.at[to % 2], fpar.at[m], c2_s.at[k], c2_r.at[k], dp, to)

    def c1(k):
        to = (dp + k) % DP
        return rc(fown.at[to % 2], cc.at[dp], c1_s.at[k], c1_r.at[k], to, m)

    def c3(k):
        to = (dp + k) % DP
        tp = to // 2
        return rc(fpar.at[tp // 2, tp % 2], rr.at[dp], c3_s.at[k], c3_r.at[k], to, m)

    for k in range(1, MP):
        c2(k).start()
    lax.fori_loop(1, DP, lambda k, v: (c1(k).start(), v)[1], 0)
    cc[dp] = fown[zl]
    fpar[m] = fown[h]
    for k in range(1, MP):
        c2(k).wait_recv()
    lax.fori_loop(1, DP, lambda k, v: (c3(k).start(), v)[1], 0)
    rr[dp] = fpar[p // 2, p % 2]
    ft = rc(fpar, fparp, ft_s, ft_r, dp, partner)
    ft.start()
    lax.fori_loop(1, DP, lambda k, v: (c3(k).wait_recv(), v)[1], 0)
    c4 = rc(rr, rrp, c4_s, c4_r, dp, partner)
    c4.start()
    ft.wait_recv()
    for q in range(MP):
        for k2 in range(2):
            col = 4 * q + 2 * k2
            feat_o[:, pl.ds(pl.multiple_of((col + h) * 128, 128), 128)] = fpar[q, k2]
            feat_o[:, pl.ds(pl.multiple_of((col + 1 - h) * 128, 128), 128)] = fparp[q, k2]
    lax.fori_loop(1, DP, lambda k, v: (c1(k).wait_recv(), v)[1], 0)

    cols = [cc[:, k2].reshape(DP * EX, 128) for k2 in range(2)]
    parts = [split(x) for x in cols]
    right = jnp.concatenate([parts[0][0], parts[1][0], parts[0][1], parts[1][1]], axis=1)

    def block(rows, par):
        lh, ll = split(rows[...].reshape(DP * EX, 128).T)
        both = dot(lh, right)
        res = both[:, 0:256] + both[:, 256:512] + dot(ll, right[:, 0:256])
        res = res * (1.0 / (DP * EX))
        for k2 in range(2):
            gb[par, :, k2] = res[:, k2 * 128 : k2 * 128 + 128].reshape(MP, 16, 128)

    block(rr, h)
    c4.wait_recv()
    block(rrp, 1 - h)

    me = zl * MP + m

    def dd(k):
        f = (me + k) % (2 * MP)
        return rc(gb.at[f // MP, f % MP], gg.at[me], dd_s.at[k], dd_r.at[k], 2 * p + f // MP, f % MP)

    for k in range(1, 2 * MP):
        dd(k).start()
    gg[me] = gb[zl, m]
    for k in range(1, 2 * MP):
        dd(k).wait_recv()
    for s in range(2 * MP):
        for k2 in range(2):
            i2 = 4 * (s % MP) + 2 * k2 + s // MP
            gram_o[:, i2 * 128 : i2 * 128 + 128] = gg[s, k2]

    for k in range(4):
        d2d[k].wait_send()
    for cp in zsend:
        cp.wait_send()
    px.wait_send()
    for cp in bs:
        cp.wait_send()
    for k in range(1, MP):
        c2(k).wait_send()
    lax.fori_loop(1, DP, lambda k, v: (c1(k).wait_send(), v)[1], 0)
    lax.fori_loop(1, DP, lambda k, v: (c3(k).wait_send(), v)[1], 0)
    c4.wait_send()
    ft.wait_send()
    for k in range(1, 2 * MP):
        dd(k).wait_send()


def body(hidden, out_grad, proj_in, proj_out, segment_ids):
    kin = hidden.shape[1]
    kout = out_grad.shape[1]
    vmem = pl.BlockSpec(memory_space=pltpu.VMEM)
    hbm = pl.BlockSpec(memory_space=pl.ANY)
    dma = pltpu.SemaphoreType.DMA
    scratch = [
        pltpu.VMEM((8, 256, kin), BF16),
        pltpu.VMEM((8, 256, kout), BF16),
        pltpu.VMEM((128, kin), BF16),
        pltpu.VMEM((128, kout), BF16),
        pltpu.VMEM((4, 256, 128), F32),
        pltpu.VMEM((4, 256, 128), F32),
        pltpu.VMEM((4, 256, 128), F32),
        pltpu.VMEM((6, 128, 128), F32),
        pltpu.VMEM((2, 128, 128), F32),
        pltpu.VMEM((256, 128), F32),
        pltpu.VMEM((256, 128), F32),
        pltpu.VMEM((256, 1024), BF16),
        pltpu.VMEM((256, 1024), BF16),
        pltpu.VMEM((1024, 256), BF16),
        pltpu.VMEM((4, 2, 2, 16, 128), F32),
        pltpu.VMEM((3, 2, 2, 16, 128), F32),
        pltpu.VMEM((2, 2, 16, 128), F32),
        pltpu.VMEM((8, 2, 16, 128), F32),
        pltpu.VMEM((8, 2, 16, 128), F32),
        pltpu.VMEM((32, 2, 16, 128), F32),
        pltpu.VMEM((32, 16, 128), F32),
        pltpu.VMEM((32, 16, 128), F32),
        pltpu.VMEM((2, 8, 2, 16, 128), F32),
        pltpu.VMEM((16, 2, 16, 128), F32),
        dma((16,)),
        dma((4,)),
        dma((4,)),
        dma((6,)),
        dma((6,)),
        dma,
        dma,
        dma((3,)),
        dma((3,)),
        dma((32,)),
        dma((32,)),
        dma((8,)),
        dma((8,)),
        dma((32,)),
        dma((32,)),
        dma,
        dma,
        dma,
        dma,
        dma((16,)),
        dma((16,)),
    ]
    return pl.pallas_call(
        kernel,
        out_shape=(
            jax.ShapeDtypeStruct((EX, 4096), F32),
            jax.ShapeDtypeStruct((16, 4096), F32),
        ),
        in_specs=[hbm, hbm, vmem, vmem, vmem],
        out_specs=(vmem, vmem),
        scratch_shapes=scratch,
        compiler_params=pltpu.CompilerParams(
            collective_id=0, has_side_effects=True, vmem_limit_bytes=40 << 20
        ),
        name="projected_gram",
    )(hidden, out_grad, proj_in, proj_out, segment_ids)


def solution(mesh):
    placed = (P("dp", "mp"), P("dp", "mp"), P(None, "mp"), P(None, "mp"), P("dp", None))
    return jax.shard_map(
        body,
        mesh=mesh,
        in_specs=placed,
        out_specs=(P("dp", None), P(("dp", "mp"), None)),
        check_vma=False,
    )
```

time: 168 us -> 76.9 us (0.46)
  waiting for transfers between devices: 92.6 us -> 0 us
  Pallas kernels: 0 us -> 61.3 us
  starting transfers between devices: 37.4 us -> 0 us
  blocking collectives: 15.9 us -> 0 us
  matrix products: 9.1 us -> 0 us
  local copies, waits for them, and re-layouts: 7.5 us -> 14.7 us
  other arithmetic: 3.43 us -> 0 us
    all_to_all x4 -> x0, waiting for transfers between devices: 92.6 us -> none  [the longest x2 60.3 us: copy_for_each(): lax.all_to_all(jnp.broadcast_to(array[None], (length, *array.shape)), axi...]
    pallas_call x0 -> x1, Pallas kernels: none -> 61.3 us  [body(): pl.pallas_call(kernel, out_shape=(jax.ShapeDtypeStruct((EX, 4096), F32),...]
    all_to_all x4 -> x0, starting transfers between devices: 37.4 us -> none  [the longest x2 14.1 us: copy_for_each(): lax.all_to_all(jnp.broadcast_to(array[None], (length, *array.shape)), axi...]
    all_to_all x1 -> x0, blocking collectives: 15.9 us -> none  [body(): lax.all_to_all(block, 'mp', split_axis=0, concat_axis=1, tiled=True)]
    unnamed x9 -> x13, local copies, waits for them, and re-layouts: 1.8 us -> 14.7 us
    dot_general x4 -> x0, matrix products: 9.1 us -> none  [the longest x1 4.4 us: body(): lax.dot_general(hidden, proj_in, (((1,), (1,)), ((), ())), preferred_elem...]
    reduce_sum x3 -> x0, other arithmetic: 3.15 us -> none  [the longest x1 1.72 us: over_copies(): return copy_for_each(array, axis).sum(axis=0)]
    broadcast_in_dim x3 -> x0, local copies, waits for them, and re-layouts: 2.84 us -> none  [copy_for_each(): jnp.broadcast_to(array[None], (length, *array.shape))]
  transfers between devices with their start and end apart: 4 -> 0, of which waited for: 4 -> 0; matrix products, arithmetic and copies ran while one was open for 0% -> 0% of each run, Pallas kernels for 0% -> 0%
where the time goes in v1:
time: 76.9 us; the launch traced here: 76.6 us
  Pallas kernels  61.3 us (80%)
  local copies, waits for them, and re-layouts  14.7 us (19%)
    pallas_call x1, Pallas kernels, body(): pl.pallas_call(kernel, out_shape=(jax.ShapeDtypeStruct((EX, 4096), F32),...  61.3 us
    unnamed x13, local copies, waits for them, and re-layouts  14.7 us

profile of v1, /device:TPU:1, one launch (start us, length us, event | category | flops | bytes accessed | tf_op | source)
XLA Modules:
  0.0 76.6 jit_solution(433787679398468507)
XLA Ops:
  0.6 0.0 copy-start.4
  0.6 0.0 copy-start.3
  0.7 0.0 copy-start.2
  0.7 0.0 copy-start.1
  0.7 10.2 %copy.7.hid = bf16[2048,1728]{1,0:T(8,128)(2,1)} copy(bf16[2048,1728]{0,1:T(8,128)(2,1)} %param.5) | data formatting | bytes 14155776 | tf_op args[0]
  10.8 0.0 copy-done.4
  10.8 0.0 copy-done.3
  10.8 0.0 copy-done.2
  10.8 0.0 copy-done.1
  10.8 0.0 copy-start
  10.9 3.1 %copy-done = bf16[2048,1728]{1,0:T(8,128)(2,1)S(1)} copy-done((bf16[2048,1728]{1,0:T(8,128)(2,1)S(1)}, bf16[2048,1728]{1,0:T(8,128)(2,1)}, u32[]{:S(2)}) %copy-start) | copy-done | bytes 7077912
  13.9 61.3 %projected_gram.1 = (f32[16,4096]{1,0:T(8,128)S(1)}, f32[16,4096]{1,0:T(8,128)S(1)}) custom-call(bf16[2048,1728]{1,0:T(8,128)(2,1)S(1)} %copy-done, bf16[2048,640]{1,0:T(8,128)(2,1)S(1)} %copy-done.1, bf16[64,1728]{1,0:T(8,128)(2,1)S(1)} %copy-done.2, bf16[64,640]{1,0:T(8,128)(2,1)S(1)} %copy-done.3, s32[1,2048]{1,0:T(1,128)S(1)} %copy-done.4), custom_call_target="tpu_custom_call" | custom-call | tf_op jit(solution)/shard_map/projected_gram/pallas_call | solution.py:381
  75.2 0.7 copy.10
  75.9 0.7 copy.11
Async XLA Ops:
  0.6 10.2 %copy-start.4 = (s32[1,2048]{1,0:T(1,128)S(1)}, s32[1,2048]{1,0:T(1,128)}, u32[]{:S(2)}) copy-start(s32[1,2048]{1,0:T(1,128)} %seg.1) | copy-start | bytes 24580
  0.6 10.2 %copy-start.3 = (bf16[64,640]{1,0:T(8,128)(2,1)S(1)}, bf16[64,640]{1,0:T(8,128)(2,1)}, u32[]{:S(2)}) copy-start(bf16[64,640]{1,0:T(8,128)(2,1)} %pout.1) | copy-start | bytes 245764
  0.7 10.2 %copy-start.2 = (bf16[64,1728]{1,0:T(8,128)(2,1)S(1)}, bf16[64,1728]{1,0:T(8,128)(2,1)}, u32[]{:S(2)}) copy-start(bf16[64,1728]{1,0:T(8,128)(2,1)} %pin.1) | copy-start | bytes 663556
  0.7 10.2 %copy-start.1 = (bf16[2048,640]{1,0:T(8,128)(2,1)S(1)}, bf16[2048,640]{1,0:T(8,128)(2,1)}, u32[]{:S(2)}) copy-start(bf16[2048,640]{1,0:T(8,128)(2,1)} %og.1) | copy-start | bytes 7864324
  10.8 3.1 %copy-start = (bf16[2048,1728]{1,0:T(8,128)(2,1)S(1)}, bf16[2048,1728]{1,0:T(8,128)(2,1)}, u32[]{:S(2)}) copy-start(bf16[2048,1728]{1,0:T(8,128)(2,1)} %copy.7.hid) | copy-start | bytes 21233668

commit v2 on v1

--- a/solution.py
+++ b/solution.py
@@ -29,15 +29,16 @@
 def kernel(
     hid,
     og,
+    pin_h,
+    pout_h,
+    seg_h,
+    feat_o,
+    gram_o,
     pin,
     pout,
     seg,
-    feat_o,
-    gram_o,
     hbuf,
     gbuf,
-    wh,
-    wg,
     psend,
     pmine,
     precv,
@@ -99,15 +100,36 @@
             device_id_type=MESH,
         )
 
+    sent = []
+
+    def drain():
+        for wait in sent:
+            wait()
+
+    def launch(copy):
+        copy.start()
+        sent.append(copy.wait_send)
+
+    def launch_each(n, f):
+        each(n, lambda k: f(k).start())
+        sent.append(lambda: each(n, lambda k: f(k).wait_send()))
+
+    def each(n, f):
+        lax.fori_loop(1, n, lambda k, v: (f(k), v)[1], 0)
+
     owners = [(c + 2) % 4, (c + 1) % 4, (c + 3) % 4, c]
     blocks = []
     for o in owners:
         blocks.append(o * 2 + (1 - h))
         blocks.append(o * 2 + h)
+    small = []
+    for k, (src, dst) in enumerate(((pin_h, pin), (pout_h, pout), (seg_h, seg))):
+        small.append(pltpu.make_async_copy(src, dst, lsem.at[16 + k]))
+        small[k].start()
     loads = []
     for k, blk in enumerate(blocks):
         rows = pl.ds(pl.multiple_of(blk * nblk, nblk), nblk)
-        a = pltpu.make_async_copy(hid.at[rows], hbuf.at[k], lsem.at[2 * k])
+        a = pltpu.make_async_copy(hid.at[:, rows], hbuf.at[k], lsem.at[2 * k])
         b = pltpu.make_async_copy(og.at[rows], gbuf.at[k], lsem.at[2 * k + 1])
         a.start()
         b.start()
@@ -130,20 +152,22 @@
 
     lax.fori_loop(1, MP, greet_own, 0)
 
-    wh[0:64, :] = pin[...]
-    wh[64:128, :] = jnp.zeros((64, wh.shape[1]), BF16)
-    wg[0:64, :] = jnp.zeros((64, wg.shape[1]), BF16)
-    wg[64:128, :] = pout[...]
-
+    rb[...] = jnp.zeros(rb.shape, BF16)
+
+    small[2].wait()
     segv = seg[...]
     erow = lax.broadcasted_iota(jnp.int32, (EX, segv.shape[1]), 0)
     counts = jnp.sum(jnp.where(erow == segv, 1.0, 0.0).astype(F32), axis=1, keepdims=True)
     scale = 1.0 / jnp.sqrt(counts)
 
-    def project(k):
+    small[0].wait()
+    small[1].wait()
+
+    def project(k, ref):
         loads[k][0].wait()
+        ref[0:64] = dot(pin[...], hbuf[k])
         loads[k][1].wait()
-        return dot_nt(hbuf[k], wh[...]) + dot_nt(gbuf[k], wg[...])
+        ref[64:128] = dot_nt(pout[...], gbuf[k])
 
     d2d = []
     zsend = []
@@ -157,61 +181,57 @@
         d2d[k].wait_recv()
         pmine[k] = pmine[k] + precv[k]
         if k == 0:
-            zsend.append(zcopy(0, pmine.at[0, 0:128], down))
-            zsend.append(zcopy(1, pmine.at[0, 128:256], up))
-            zsend[0].start()
-            zsend[1].start()
+            zsend.append(zcopy(0, pmine.at[0, 0:64], down))
+            zsend.append(zcopy(1, pmine.at[0, 64:128], up))
+            launch(zsend[0])
+            launch(zsend[1])
         if k == 1:
-            zsend.append(zcopy(2, pmine.at[1, 0:128], up))
-            zsend[2].start()
+            zsend.append(zcopy(2, pmine.at[1, 0:64], up))
+            launch(zsend[2])
         if k == 2:
-            zsend.append(zcopy(3, pmine.at[2, 128:256], down))
-            zsend[3].start()
+            zsend.append(zcopy(3, pmine.at[2, 64:128], down))
+            launch(zsend[3])
 
     for k in range(4):
-        psend[k] = project(2 * k)
+        project(2 * k, psend.at[k])
         if k == 0:
             pl.semaphore_wait(barrier, DP - 1 + 2 * (MP - 1))
         d2d.append(rc(psend.at[k], precv.at[k], d2d_s.at[k], d2d_r.at[k], dp, partner))
-        d2d[k].start()
-        pmine[k] = project(2 * k + 1)
+        launch(d2d[k])
+        project(2 * k + 1, pmine.at[k])
         if k >= 1:
             finish(k - 1)
     finish(3)
 
     zsend[0].wait_recv()
-    zrel[0] = zrecv[0] + pmine[2, 0:128]
+    zrel[0] = zrecv[0] + pmine[2, 0:64]
     zsend.append(zcopy(4, zrel.at[0], down))
-    zsend[4].start()
+    launch(zsend[4])
     zsend[1].wait_recv()
-    zrel[1] = zrecv[1] + pmine[1, 128:256]
+    zrel[1] = zrecv[1] + pmine[1, 64:128]
     zsend.append(zcopy(5, zrel.at[1], up))
-    zsend[5].start()
+    launch(zsend[5])
     zsend[2].wait_recv()
     zsend[3].wait_recv()
     zsend[4].wait_recv()
     zsend[5].wait_recv()
-    pown[0:128] = pmine[3, 0:128] + zrecv[2] + zrecv[4]
-    pown[128:256] = pmine[3, 128:256] + zrecv[3] + zrecv[5]
+    pown[0:64] = pmine[3, 0:64] + zrecv[2] + zrecv[4]
+    pown[64:128] = pmine[3, 64:128] + zrecv[3] + zrecv[5]
 
     px = rc(pown, ppart, px_s, px_r, dp, partner)
-    px.start()
+    launch(px)
 
     def weigh(s, toks, blk):
-        low = jnp.where(lax.broadcasted_iota(jnp.int32, (nblk, 128), 1) < 64, toks, 0.0)
-        high = pltpu.roll(low, 64, 1)
-        lh, ll = split(low)
-        hh, hl = split(high)
+        ih, il = split(toks[0:64])
         base = s * 512
-        rb[base : base + 256, 0:128] = lh
-        rb[base : base + 256, 128:256] = ll
-        rb[base + 256 : base + 512, 0:128] = hh
-        rb[base + 256 : base + 512, 128:256] = hl
-        trans = toks.T
+        rb[0:64, base : base + 256] = ih
+        rb[64:128, base + 256 : base + 512] = ih
+        rb[128:192, base : base + 256] = il
+        rb[192:256, base + 256 : base + 512] = il
         ids = seg[:, pl.ds(pl.multiple_of(blk * nblk, nblk), nblk)]
         mask = lax.broadcasted_iota(jnp.int32, (EX, nblk), 0) == ids
         for cq in range(4):
-            rows = jnp.where(h == 0, trans[64 + 16 * cq : 72 + 16 * cq], trans[72 + 16 * cq : 80 + 16 * cq])
+            rows = toks[pl.ds(pl.multiple_of(64 + 16 * cq + 8 * h, 8), 8)]
             for k in range(4):
                 tile = (cq * 2 + k % 2) * 2 + k // 2
                 for par in range(2):
@@ -222,20 +242,20 @@
 
     def grads(s):
         cols = slice(s * 512, s * 512 + 512)
-        both = dot(whi[:, cols], rb[cols, :])
-        return both[:, 0:128] + both[:, 128:256] + dot(wlo[:, cols], rb[cols, 0:128])
-
-    weigh(0, pown[...], m)
+        both = dot_nt(whi[:, cols], rb[:, cols])
+        return both[:, 0:128] + both[:, 128:256] + dot_nt(wlo[:, cols], rb[0:128, cols])
+
+    weigh(0, pown, m)
     g0 = grads(0)
     px.wait_recv()
-    weigh(1, ppart[...], partner)
+    weigh(1, ppart, partner)
     gbuf2[...] = (g0 + grads(1)).reshape(4, 2, 2, 16, 128)
 
     bs = []
     for k in (2, 1, 3):
         to = (c + k) % 4
         cp = rc(gbuf2.at[to], brecv.at[k - 1], b_s.at[k - 1], b_r.at[k - 1], dp, to * 2 + h)
-        cp.start()
+        launch(cp)
         bs.append(cp)
     for cp in bs:
         cp.wait_recv()
@@ -255,26 +275,26 @@
         return rc(fpar.at[tp // 2, tp % 2], rr.at[dp], c3_s.at[k], c3_r.at[k], to, m)
 
     for k in range(1, MP):
-        c2(k).start()
-    lax.fori_loop(1, DP, lambda k, v: (c1(k).start(), v)[1], 0)
+        launch(c2(k))
+    launch_each(DP, c1)
     cc[dp] = fown[zl]
     fpar[m] = fown[h]
     for k in range(1, MP):
         c2(k).wait_recv()
-    lax.fori_loop(1, DP, lambda k, v: (c3(k).start(), v)[1], 0)
+    launch_each(DP, c3)
     rr[dp] = fpar[p // 2, p % 2]
     ft = rc(fpar, fparp, ft_s, ft_r, dp, partner)
-    ft.start()
-    lax.fori_loop(1, DP, lambda k, v: (c3(k).wait_recv(), v)[1], 0)
+    launch(ft)
+    each(DP, lambda k: c3(k).wait_recv())
     c4 = rc(rr, rrp, c4_s, c4_r, dp, partner)
-    c4.start()
+    launch(c4)
     ft.wait_recv()
     for q in range(MP):
         for k2 in range(2):
             col = 4 * q + 2 * k2
             feat_o[:, pl.ds(pl.multiple_of((col + h) * 128, 128), 128)] = fpar[q, k2]
             feat_o[:, pl.ds(pl.multiple_of((col + 1 - h) * 128, 128), 128)] = fparp[q, k2]
-    lax.fori_loop(1, DP, lambda k, v: (c1(k).wait_recv(), v)[1], 0)
+    each(DP, lambda k: c1(k).wait_recv())
 
     cols = [cc[:, k2].reshape(DP * EX, 128) for k2 in range(2)]
     parts = [split(x) for x in cols]
@@ -299,7 +319,7 @@
         return rc(gb.at[f // MP, f % MP], gg.at[me], dd_s.at[k], dd_r.at[k], 2 * p + f // MP, f % MP)
 
     for k in range(1, 2 * MP):
-        dd(k).start()
+        launch(dd(k))
     gg[me] = gb[zl, m]
     for k in range(1, 2 * MP):
         dd(k).wait_recv()
@@ -307,45 +327,32 @@
         for k2 in range(2):
             i2 = 4 * (s % MP) + 2 * k2 + s // MP
             gram_o[:, i2 * 128 : i2 * 128 + 128] = gg[s, k2]
-
-    for k in range(4):
-        d2d[k].wait_send()
-    for cp in zsend:
-        cp.wait_send()
-    px.wait_send()
-    for cp in bs:
-        cp.wait_send()
-    for k in range(1, MP):
-        c2(k).wait_send()
-    lax.fori_loop(1, DP, lambda k, v: (c1(k).wait_send(), v)[1], 0)
-    lax.fori_loop(1, DP, lambda k, v: (c3(k).wait_send(), v)[1], 0)
-    c4.wait_send()
-    ft.wait_send()
-    for k in range(1, 2 * MP):
-        dd(k).wait_send()
+    drain()
 
 
 def body(hidden, out_grad, proj_in, proj_out, segment_ids):
-    kin = hidden.shape[1]
+    hidden = hidden.T
+    kin = hidden.shape[0]
     kout = out_grad.shape[1]
     vmem = pl.BlockSpec(memory_space=pltpu.VMEM)
-    hbm = pl.BlockSpec(memory_space=pl.ANY)
+    hbm = pl.BlockSpec(memory_space=pltpu.HBM)
     dma = pltpu.SemaphoreType.DMA
     scratch = [
-        pltpu.VMEM((8, 256, kin), BF16),
+        pltpu.VMEM(proj_in.shape, BF16),
+        pltpu.VMEM(proj_out.shape, BF16),
+        pltpu.VMEM(segment_ids.shape, jnp.int32),
+        pltpu.VMEM((8, kin, 256), BF16),
         pltpu.VMEM((8, 256, kout), BF16),
-        pltpu.VMEM((128, kin), BF16),
-        pltpu.VMEM((128, kout), BF16),
-        pltpu.VMEM((4, 256, 128), F32),
-        pltpu.VMEM((4, 256, 128), F32),
-        pltpu.VMEM((4, 256, 128), F32),
-        pltpu.VMEM((6, 128, 128), F32),
-        pltpu.VMEM((2, 128, 128), F32),
-        pltpu.VMEM((256, 128), F32),
-        pltpu.VMEM((256, 128), F32),
+        pltpu.VMEM((4, 128, 256), F32),
+        pltpu.VMEM((4, 128, 256), F32),
+        pltpu.VMEM((4, 128, 256), F32),
+        pltpu.VMEM((6, 64, 256), F32),
+        pltpu.VMEM((2, 64, 256), F32),
+        pltpu.VMEM((128, 256), F32),
+        pltpu.VMEM((128, 256), F32),
         pltpu.VMEM((256, 1024), BF16),
         pltpu.VMEM((256, 1024), BF16),
-        pltpu.VMEM((1024, 256), BF16),
+        pltpu.VMEM((256, 1024), BF16),
         pltpu.VMEM((4, 2, 2, 16, 128), F32),
         pltpu.VMEM((3, 2, 2, 16, 128), F32),
         pltpu.VMEM((2, 2, 16, 128), F32),
@@ -356,7 +363,7 @@
         pltpu.VMEM((32, 16, 128), F32),
         pltpu.VMEM((2, 8, 2, 16, 128), F32),
         pltpu.VMEM((16, 2, 16, 128), F32),
-        dma((16,)),
+        dma((19,)),
         dma((4,)),
         dma((4,)),
         dma((6,)),
@@ -384,11 +391,11 @@
             jax.ShapeDtypeStruct((EX, 4096), F32),
             jax.ShapeDtypeStruct((16, 4096), F32),
         ),
-        in_specs=[hbm, hbm, vmem, vmem, vmem],
+        in_specs=[hbm, hbm, hbm, hbm, hbm],
         out_specs=(vmem, vmem),
         scratch_shapes=scratch,
         compiler_params=pltpu.CompilerParams(
-            collective_id=0, has_side_effects=True, vmem_limit_bytes=40 << 20
+            collective_id=0, has_side_effects=True, vmem_limit_bytes=65800000
         ),
         name="projected_gram",
     )(hidden, out_grad, proj_in, proj_out, segment_ids)

time: 76.9 us -> 63.8 us (0.83)
  local copies, waits for them, and re-layouts: 14.7 us -> 3.34 us
  Pallas kernels: 61.3 us -> 59.7 us
    unnamed x13 -> x2, local copies, waits for them, and re-layouts: 14.7 us -> 3.34 us
    pallas_call x1, Pallas kernels: 61.3 us -> 59.7 us  [body(): pl.pallas_call(kernel, out_shape=(jax.ShapeDtypeStruct((EX, 4096), F32),...]
where the time goes in v2:
time: 63.8 us; the launch traced here: 63.7 us
  Pallas kernels  59.7 us (94%)
  local copies, waits for them, and re-layouts  3.34 us (5%)
  between operations  0.64 us (1%)
    pallas_call x1, Pallas kernels, body(): pl.pallas_call(kernel, out_shape=(jax.ShapeDtypeStruct((EX, 4096), F32),...  59.7 us
    unnamed x2, local copies, waits for them, and re-layouts  3.34 us

profile of v2, /device:TPU:1, one launch (start us, length us, event | category | flops | bytes accessed | tf_op | source)
XLA Modules:
  0.0 63.7 jit_solution(3583394985905095491)
XLA Ops:
  0.6 59.7 %projected_gram.1 = (f32[16,4096]{1,0:T(8,128)}, f32[16,4096]{1,0:T(8,128)}) custom-call(bf16[1728,2048]{1,0:T(8,128)(2,1)} %bitcast.1, bf16[2048,640]{1,0:T(8,128)(2,1)} %og.1, bf16[64,1728]{1,0:T(8,128)(2,1)} %pin_h.1, bf16[64,640]{1,0:T(8,128)(2,1)} %pout_h.1, s32[1,2048]{1,0:T(1,128)} %seg_h.1), custom_call_target="tpu_custom_call" | custom-call | tf_op jit(solution)/shard_map/projected_gram/pallas_call | solution.py:388
  60.3 1.7 %copy.9 = f32[16,4096]{1,0:T(8,128)} copy(f32[16,4096]{1,0:T(8,128)} %get-tuple-element.4) | data formatting | bytes 524288
  62.0 1.7 %copy.10 = f32[16,4096]{1,0:T(8,128)} copy(f32[16,4096]{1,0:T(8,128)} %get-tuple-element.5) | data formatting | bytes 524288

commit v3 on v2

--- a/solution.py
+++ b/solution.py
@@ -9,6 +9,7 @@
 EX = 16
 DP = 32
 MP = 8
+XY = 16
 F32 = jnp.float32
 BF16 = jnp.bfloat16
 
@@ -53,10 +54,13 @@
     brecv,
     fown,
     fpar,
-    fparp,
+    fnat,
+    fnatp,
     cc,
+    ccp,
     rr,
-    rrp,
+    ath,
+    atl,
     gb,
     gg,
     lsem,
@@ -145,12 +149,17 @@
 
     def greet_own(k, carry):
         pl.semaphore_signal(barrier, inc=1, device_id=(dp, (m + k) % MP), device_id_type=MESH)
+        return carry
+
+    lax.fori_loop(1, MP, greet_own, 0)
+
+    def greet_plane(k, carry):
         pl.semaphore_signal(
-            barrier, inc=1, device_id=(2 * p + (1 - zl), (m + k) % MP), device_id_type=MESH
+            barrier, inc=1, device_id=((p + k) % XY * 2 + zl, partner), device_id_type=MESH
         )
         return carry
 
-    lax.fori_loop(1, MP, greet_own, 0)
+    lax.fori_loop(1, XY, greet_plane, 0)
 
     rb[...] = jnp.zeros(rb.shape, BF16)
 
@@ -195,7 +204,7 @@
     for k in range(4):
         project(2 * k, psend.at[k])
         if k == 0:
-            pl.semaphore_wait(barrier, DP - 1 + 2 * (MP - 1))
+            pl.semaphore_wait(barrier, DP - 1 + MP - 1 + XY - 1)
         d2d.append(rc(psend.at[k], precv.at[k], d2d_s.at[k], d2d_r.at[k], dp, partner))
         launch(d2d[k])
         project(2 * k + 1, pmine.at[k])
@@ -230,15 +239,13 @@
         rb[192:256, base + 256 : base + 512] = il
         ids = seg[:, pl.ds(pl.multiple_of(blk * nblk, nblk), nblk)]
         mask = lax.broadcasted_iota(jnp.int32, (EX, nblk), 0) == ids
-        for cq in range(4):
-            rows = toks[pl.ds(pl.multiple_of(64 + 16 * cq + 8 * h, 8), 8)]
-            for k in range(4):
-                tile = (cq * 2 + k % 2) * 2 + k // 2
-                for par in range(2):
-                    one = jnp.where(mask, rows[2 * k + par : 2 * k + par + 1, :], 0.0)
-                    oh, ol = split(one)
-                    whi[tile * 16 : tile * 16 + 16, base + par * 256 : base + par * 256 + 256] = oh
-                    wlo[tile * 16 : tile * 16 + 16, base + par * 256 : base + par * 256 + 256] = ol
+        rows = toks[pl.ds(pl.multiple_of(64 + 32 * h, 32), 32)]
+        for t in range(16):
+            for par in range(2):
+                one = jnp.where(mask, rows[2 * t + par : 2 * t + par + 1, :], 0.0)
+                oh, ol = split(one)
+                whi[t * 16 : t * 16 + 16, base + par * 256 : base + par * 256 + 256] = oh
+                wlo[t * 16 : t * 16 + 16, base + par * 256 : base + par * 256 + 256] = ol
 
     def grads(s):
         cols = slice(s * 512, s * 512 + 512)
@@ -249,7 +256,20 @@
     g0 = grads(0)
     px.wait_recv()
     weigh(1, ppart, partner)
-    gbuf2[...] = (g0 + grads(1)).reshape(4, 2, 2, 16, 128)
+    nat = (g0 + grads(1)).reshape(16, EX, 128)
+    group = lax.broadcasted_iota(jnp.int32, (EX, 128), 1) // 32
+
+    def regroup(tiles, here):
+        out = None
+        for g in range(4):
+            moved = tiles[g] if g == here else pltpu.roll(tiles[g], 32 * ((g - here) % 4), 1)
+            out = moved if out is None else jnp.where(group == g, moved, out)
+        return out
+
+    for cq in range(4):
+        for z in range(2):
+            for k in range(2):
+                gbuf2[cq, z, k] = regroup([nat[8 * k + 2 * g + z] for g in range(4)], cq)
 
     bs = []
     for k in (2, 1, 3):
@@ -261,72 +281,96 @@
         cp.wait_recv()
     fown[...] = (gbuf2[c] + brecv[0] + brecv[1] + brecv[2]) * scale[None, None]
 
+    other = 2 * p + 1 - zl
+
     def c2(k):
         to = (m + k) % MP
         return rc(fown.at[to % 2], fpar.at[m], c2_s.at[k], c2_r.at[k], dp, to)
 
     def c1(k):
-        to = (dp + k) % DP
-        return rc(fown.at[to % 2], cc.at[dp], c1_s.at[k], c1_r.at[k], to, m)
+        to = (p + k) % XY * 2 + zl
+        return rc(fown.at[zl], cc.at[zl, p], c1_s.at[k], c1_r.at[k], to, m)
+
+    def c1b(k):
+        to = (p + k) % XY * 2 + zl
+        mid = cc.at[1 - zl, p]
+        return rc(mid, mid, c1_s.at[16 + k], c1_r.at[16 + k], to, m)
 
     def c3(k):
         to = (dp + k) % DP
-        tp = to // 2
-        return rc(fpar.at[tp // 2, tp % 2], rr.at[dp], c3_s.at[k], c3_r.at[k], to, m)
+        return rc(fnat.at[to // 2], rr.at[zl, p], c3_s.at[k], c3_r.at[k], to, m)
 
     for k in range(1, MP):
         launch(c2(k))
-    launch_each(DP, c1)
-    cc[dp] = fown[zl]
+    x1 = rc(fown.at[1 - zl], cc.at[zl, p], c1_s.at[0], c1_r.at[0], other, m)
+    launch(x1)
+    launch_each(XY, c1)
+    cc[zl, p] = fown[zl]
     fpar[m] = fown[h]
+    x1.wait_recv()
+    launch_each(XY, c1b)
     for k in range(1, MP):
         c2(k).wait_recv()
+    for q in range(4):
+        for g in range(4):
+            fnat[4 * q + g] = regroup([fpar[2 * cq + q // 2, q % 2] for cq in range(4)], g)
     launch_each(DP, c3)
-    rr[dp] = fpar[p // 2, p % 2]
-    ft = rc(fpar, fparp, ft_s, ft_r, dp, partner)
+    rr[zl, p] = fnat[p]
+    ft = rc(fnat, fnatp, ft_s, ft_r, dp, partner)
     launch(ft)
+
+    def swap(z):
+        return rc(cc.at[z], ccp.at[z], c4_s.at[z], c4_r.at[z], dp, partner)
+
+    each(XY, lambda k: c1(k).wait_recv())
+    launch(swap(zl))
+    each(XY, lambda k: c1b(k).wait_recv())
+    launch(swap(1 - zl))
+    ft.wait_recv()
+    for q in range(XY):
+        feat_o[:, pl.ds(pl.multiple_of((2 * q + h) * 128, 128), 128)] = fnat[q]
+        feat_o[:, pl.ds(pl.multiple_of((2 * q + 1 - h) * 128, 128), 128)] = fnatp[q]
+
+    def turned(ref, side):
+        for k in range(2):
+            for z in range(2):
+                hi, lo = split(ref[z, :, k].reshape(XY * EX, 128).T)
+                ath[side, k * 128 : k * 128 + 128, z * 256 : z * 256 + 256] = hi
+                atl[side, k * 128 : k * 128 + 128, z * 256 : z * 256 + 256] = lo
+
+    turned(cc, 0)
+    swap(zl).wait_recv()
+    swap(1 - zl).wait_recv()
+    turned(ccp, 1)
     each(DP, lambda k: c3(k).wait_recv())
-    c4 = rc(rr, rrp, c4_s, c4_r, dp, partner)
-    launch(c4)
-    ft.wait_recv()
-    for q in range(MP):
-        for k2 in range(2):
-            col = 4 * q + 2 * k2
-            feat_o[:, pl.ds(pl.multiple_of((col + h) * 128, 128), 128)] = fpar[q, k2]
-            feat_o[:, pl.ds(pl.multiple_of((col + 1 - h) * 128, 128), 128)] = fparp[q, k2]
-    each(DP, lambda k: c1(k).wait_recv())
-
-    cols = [cc[:, k2].reshape(DP * EX, 128) for k2 in range(2)]
-    parts = [split(x) for x in cols]
-    right = jnp.concatenate([parts[0][0], parts[1][0], parts[0][1], parts[1][1]], axis=1)
-
-    def block(rows, par):
-        lh, ll = split(rows[...].reshape(DP * EX, 128).T)
-        both = dot(lh, right)
-        res = both[:, 0:256] + both[:, 256:512] + dot(ll, right[:, 0:256])
-        res = res * (1.0 / (DP * EX))
-        for k2 in range(2):
-            gb[par, :, k2] = res[:, k2 * 128 : k2 * 128 + 128].reshape(MP, 16, 128)
-
-    block(rr, h)
-    c4.wait_recv()
-    block(rrp, 1 - h)
-
-    me = zl * MP + m
+    rh, rl = split(rr[...].reshape(DP * EX, 128))
+    right = jnp.concatenate([rh, rl], axis=1)
+    for side in range(2):
+        both = dot(ath[side], right)
+        res = both[:, 0:128] + both[:, 128:256] + dot(atl[side], rh)
+        res = (res * (1.0 / (DP * EX))).reshape(2, 4, 2, 16, 128)
+        first = h if side == 0 else 1 - h
+        gb[pl.ds(2 * first, 2)] = res
+
+    me = 2 * p + h
 
     def dd(k):
-        f = (me + k) % (2 * MP)
-        return rc(gb.at[f // MP, f % MP], gg.at[me], dd_s.at[k], dd_r.at[k], 2 * p + f // MP, f % MP)
-
-    for k in range(1, 2 * MP):
-        launch(dd(k))
-    gg[me] = gb[zl, m]
-    for k in range(1, 2 * MP):
-        dd(k).wait_recv()
-    for s in range(2 * MP):
-        for k2 in range(2):
-            i2 = 4 * (s % MP) + 2 * k2 + s // MP
-            gram_o[:, i2 * 128 : i2 * 128 + 128] = gg[s, k2]
+        f = (me + k) % DP
+        return rc(
+            gb.at[f // 8, f // 2 % 4, f % 2],
+            gg.at[me],
+            dd_s.at[k],
+            dd_r.at[k],
+            f // 2 * 2 + zl,
+            2 * c + f % 2,
+        )
+
+    launch_each(DP, dd)
+    gg[me] = gb[p // 4, p % 4, h]
+    each(DP, lambda k: dd(k).wait_recv())
+    for i in range(DP):
+        gram_o[:, i * 128 : i * 128 + 128] = gg[i]
+
     drain()
 
 
@@ -357,12 +401,15 @@
         pltpu.VMEM((3, 2, 2, 16, 128), F32),
         pltpu.VMEM((2, 2, 16, 128), F32),
         pltpu.VMEM((8, 2, 16, 128), F32),
-        pltpu.VMEM((8, 2, 16, 128), F32),
-        pltpu.VMEM((32, 2, 16, 128), F32),
+        pltpu.VMEM((16, 16, 128), F32),
+        pltpu.VMEM((16, 16, 128), F32),
+        pltpu.VMEM((2, 16, 2, 16, 128), F32),
+        pltpu.VMEM((2, 16, 2, 16, 128), F32),
+        pltpu.VMEM((2, 16, 16, 128), F32),
+        pltpu.VMEM((2, 256, 512), BF16),
+        pltpu.VMEM((2, 256, 512), BF16),
+        pltpu.VMEM((4, 4, 2, 16, 128), F32),
         pltpu.VMEM((32, 16, 128), F32),
-        pltpu.VMEM((32, 16, 128), F32),
-        pltpu.VMEM((2, 8, 2, 16, 128), F32),
-        pltpu.VMEM((16, 2, 16, 128), F32),
         dma((19,)),
         dma((4,)),
         dma((4,)),
@@ -378,12 +425,12 @@
         dma((8,)),
         dma((32,)),
         dma((32,)),
+        dma((2,)),
+        dma((2,)),
         dma,
         dma,
-        dma,
-        dma,
-        dma((16,)),
-        dma((16,)),
+        dma((32,)),
+        dma((32,)),
     ]
     return pl.pallas_call(
         kernel,

time: 63.8 us -> 60.7 us (0.951)
  Pallas kernels: 59.7 us -> 56.6 us
    pallas_call x1, Pallas kernels: 59.7 us -> 56.6 us  [body(): pl.pallas_call(kernel, out_shape=(jax.ShapeDtypeStruct((EX, 4096), F32),...]
where the time goes in v3:
time: 60.7 us; the launch traced here: 60.6 us
  Pallas kernels  56.6 us (93%)
  local copies, waits for them, and re-layouts  3.34 us (6%)
  between operations  0.64 us (1%)
    pallas_call x1, Pallas kernels, body(): pl.pallas_call(kernel, out_shape=(jax.ShapeDtypeStruct((EX, 4096), F32),...  56.6 us
    unnamed x2, local copies, waits for them, and re-layouts  3.34 us

profile of v3, /device:TPU:1, one launch (start us, length us, event | category | flops | bytes accessed | tf_op | source)
XLA Modules:
  0.0 60.6 jit_solution(6946431243718475295)
XLA Ops:
  0.6 56.6 %projected_gram.1 = (f32[16,4096]{1,0:T(8,128)}, f32[16,4096]{1,0:T(8,128)}) custom-call(bf16[1728,2048]{1,0:T(8,128)(2,1)} %bitcast.1, bf16[2048,640]{1,0:T(8,128)(2,1)} %og.1, bf16[64,1728]{1,0:T(8,128)(2,1)} %pin_h.1, bf16[64,640]{1,0:T(8,128)(2,1)} %pout_h.1, s32[1,2048]{1,0:T(1,128)} %seg_h.1), custom_call_target="tpu_custom_call" | custom-call | tf_op jit(solution)/shard_map/projected_gram/pallas_call | solution.py:435
  57.3 1.7 %copy.9 = f32[16,4096]{1,0:T(8,128)} copy(f32[16,4096]{1,0:T(8,128)} %get-tuple-element.4) | data formatting | bytes 524288
  58.9 1.7 %copy.10 = f32[16,4096]{1,0:T(8,128)} copy(f32[16,4096]{1,0:T(8,128)} %get-tuple-element.5) | data formatting | bytes 524288

commit v4 on v3

--- a/solution.py
+++ b/solution.py
@@ -281,40 +281,75 @@
         cp.wait_recv()
     fown[...] = (gbuf2[c] + brecv[0] + brecv[1] + brecv[2]) * scale[None, None]
 
-    other = 2 * p + 1 - zl
+    far = (2, 1, 3, 0)
+    yy = p // 4
+    xx = p % 4
+    u = yy * (1 - h) + xx * h
+    v = xx * (1 - h) + yy * h
+
+    def spot(first, second):
+        return (first * (4 - 3 * h) + second * (1 + 3 * h)) * 2 + zl
 
     def c2(k):
         to = (m + k) % MP
         return rc(fown.at[to % 2], fpar.at[m], c2_s.at[k], c2_r.at[k], dp, to)
 
-    def c1(k):
-        to = (p + k) % XY * 2 + zl
-        return rc(fown.at[zl], cc.at[zl, p], c1_s.at[k], c1_r.at[k], to, m)
-
-    def c1b(k):
-        to = (p + k) % XY * 2 + zl
-        mid = cc.at[1 - zl, p]
-        return rc(mid, mid, c1_s.at[16 + k], c1_r.at[16 + k], to, m)
+    def near(z, k):
+        src = fown.at[zl] if z == 0 else cc.at[1 - zl, u, v]
+        dst = cc.at[(zl + z) % 2, u, v]
+        n = 1 + z * 6 + k
+        return rc(src, dst, c1_s.at[n], c1_r.at[n], spot(u, (v + k) % 4), m)
+
+    def wide(z, k):
+        row = cc.at[(zl + z) % 2, u]
+        n = 4 + z * 6 + k
+        return rc(row, row, c1_s.at[n], c1_r.at[n], spot((u + k) % 4, v), m)
 
     def c3(k):
-        to = (dp + k) % DP
-        return rc(fnat.at[to // 2], rr.at[zl, p], c3_s.at[k], c3_r.at[k], to, m)
-
-    for k in range(1, MP):
+        tp = (yy + k // 8) % 4 * 4 + (xx + k // 2 % 4) % 4
+        to = tp * 2 + (zl + k % 2) % 2
+        return rc(fnat.at[tp], rr.at[zl, p], c3_s.at[k], c3_r.at[k], to, m)
+
+    def dd(k):
+        ty = (yy + k // 8) % 4
+        tx = (xx + k // 2 % 4) % 4
+        th = (h + k % 2) % 2
+        return rc(
+            gb.at[ty, tx, th],
+            gg.at[2 * p + h],
+            dd_s.at[k],
+            dd_r.at[k],
+            (ty * 4 + tx) * 2 + zl,
+            2 * c + th,
+        )
+
+    for k in (4, 5, 3, 2, 6, 7, 1):
         launch(c2(k))
-    x1 = rc(fown.at[1 - zl], cc.at[zl, p], c1_s.at[0], c1_r.at[0], other, m)
+    x1 = rc(fown.at[1 - zl], cc.at[zl, u, v], c1_s.at[0], c1_r.at[0], 2 * p + 1 - zl, m)
     launch(x1)
-    launch_each(XY, c1)
-    cc[zl, p] = fown[zl]
+    for k in far[:3]:
+        launch(near(0, k))
+    cc[zl, u, v] = fown[zl]
     fpar[m] = fown[h]
     x1.wait_recv()
-    launch_each(XY, c1b)
+    for k in far[:3]:
+        launch(near(1, k))
+    for z in range(2):
+        for k in far[:3]:
+            near(z, k).wait_recv()
+        for k in far[:3]:
+            launch(wide(z, k))
     for k in range(1, MP):
         c2(k).wait_recv()
     for q in range(4):
         for g in range(4):
             fnat[4 * q + g] = regroup([fpar[2 * cq + q // 2, q % 2] for cq in range(4)], g)
-    launch_each(DP, c3)
+    for dz in (1, 0):
+        for dy in far:
+            for dx in far:
+                if dy + dx + dz:
+                    c3(dy * 8 + dx * 2 + dz).start()
+    sent.append(lambda: each(DP, lambda k: c3(k).wait_send()))
     rr[zl, p] = fnat[p]
     ft = rc(fnat, fnatp, ft_s, ft_r, dp, partner)
     launch(ft)
@@ -322,51 +357,46 @@
     def swap(z):
         return rc(cc.at[z], ccp.at[z], c4_s.at[z], c4_r.at[z], dp, partner)
 
-    each(XY, lambda k: c1(k).wait_recv())
-    launch(swap(zl))
-    each(XY, lambda k: c1b(k).wait_recv())
-    launch(swap(1 - zl))
+    for z in range(2):
+        for k in far[:3]:
+            wide(z, k).wait_recv()
+        launch(swap((zl + z) % 2))
     ft.wait_recv()
     for q in range(XY):
         feat_o[:, pl.ds(pl.multiple_of((2 * q + h) * 128, 128), 128)] = fnat[q]
         feat_o[:, pl.ds(pl.multiple_of((2 * q + 1 - h) * 128, 128), 128)] = fnatp[q]
 
-    def turned(ref, side):
+    def turned(ref, core):
         for k in range(2):
             for z in range(2):
-                hi, lo = split(ref[z, :, k].reshape(XY * EX, 128).T)
-                ath[side, k * 128 : k * 128 + 128, z * 256 : z * 256 + 256] = hi
-                atl[side, k * 128 : k * 128 + 128, z * 256 : z * 256 + 256] = lo
-
-    turned(cc, 0)
+                tiles = []
+                for y in range(4):
+                    for x in range(4):
+                        first = y * (1 - core) + x * core
+                        second = x * (1 - core) + y * core
+                        tiles.append(ref[z, first, second, k])
+                hi, lo = split(jnp.concatenate(tiles, axis=0).T)
+                ath[2 * core + k, :, z * 256 : z * 256 + 256] = hi
+                atl[2 * core + k, :, z * 256 : z * 256 + 256] = lo
+
+    turned(cc, h)
     swap(zl).wait_recv()
     swap(1 - zl).wait_recv()
-    turned(ccp, 1)
+    turned(ccp, 1 - h)
     each(DP, lambda k: c3(k).wait_recv())
     rh, rl = split(rr[...].reshape(DP * EX, 128))
     right = jnp.concatenate([rh, rl], axis=1)
-    for side in range(2):
-        both = dot(ath[side], right)
-        res = both[:, 0:128] + both[:, 128:256] + dot(atl[side], rh)
-        res = (res * (1.0 / (DP * EX))).reshape(2, 4, 2, 16, 128)
-        first = h if side == 0 else 1 - h
-        gb[pl.ds(2 * first, 2)] = res
-
-    me = 2 * p + h
-
-    def dd(k):
-        f = (me + k) % DP
-        return rc(
-            gb.at[f // 8, f // 2 % 4, f % 2],
-            gg.at[me],
-            dd_s.at[k],
-            dd_r.at[k],
-            f // 2 * 2 + zl,
-            2 * c + f % 2,
-        )
-
-    launch_each(DP, dd)
-    gg[me] = gb[p // 4, p % 4, h]
+    for dy in far:
+        q = (yy + dy) % 4
+        both = dot(ath[q], right)
+        res = both[:, 0:128] + both[:, 128:256] + dot(atl[q], rh)
+        gb[q] = (res * (1.0 / (DP * EX))).reshape(4, 2, 16, 128)
+        for dx in far:
+            for dh in (1, 0):
+                if dy + dx + dh:
+                    dd(dy * 8 + dx * 2 + dh).start()
+    sent.append(lambda: each(DP, lambda k: dd(k).wait_send()))
+    gg[2 * p + h] = gb[yy, xx, h]
     each(DP, lambda k: dd(k).wait_recv())
     for i in range(DP):
         gram_o[:, i * 128 : i * 128 + 128] = gg[i]
@@ -403,11 +433,11 @@
         pltpu.VMEM((8, 2, 16, 128), F32),
         pltpu.VMEM((16, 16, 128), F32),
         pltpu.VMEM((16, 16, 128), F32),
-        pltpu.VMEM((2, 16, 2, 16, 128), F32),
-        pltpu.VMEM((2, 16, 2, 16, 128), F32),
+        pltpu.VMEM((2, 4, 4, 2, 16, 128), F32),
+        pltpu.VMEM((2, 4, 4, 2, 16, 128), F32),
         pltpu.VMEM((2, 16, 16, 128), F32),
-        pltpu.VMEM((2, 256, 512), BF16),
-        pltpu.VMEM((2, 256, 512), BF16),
+        pltpu.VMEM((4, 128, 512), BF16),
+        pltpu.VMEM((4, 128, 512), BF16),
         pltpu.VMEM((4, 4, 2, 16, 128), F32),
         pltpu.VMEM((32, 16, 128), F32),
         dma((19,)),
@@ -435,8 +465,8 @@
     return pl.pallas_call(
         kernel,
         out_shape=(
-            jax.ShapeDtypeStruct((EX, 4096), F32),
-            jax.ShapeDtypeStruct((16, 4096), F32),
+            pltpu.VMEM((EX, 4096), F32),
+            pltpu.VMEM((16, 4096), F32),
         ),
         in_specs=[hbm, hbm, hbm, hbm, hbm],
         out_specs=(vmem, vmem),

time: 60.7 us -> 59.1 us (0.974)
  local copies, waits for them, and re-layouts: 3.34 us -> 1.41 us
    unnamed x2, local copies, waits for them, and re-layouts: 3.34 us -> 1.41 us
where the time goes in v4:
time: 59.1 us; the launch traced here: 59 us
  Pallas kernels  57 us (96%)
  local copies, waits for them, and re-layouts  1.41 us (2%)
  between operations  0.64 us (1%)
    pallas_call x1, Pallas kernels, body(): pl.pallas_call(kernel, out_shape=(pltpu.VMEM((EX, 4096), F32), pltpu.VMEM...  57 us
    unnamed x2, local copies, waits for them, and re-layouts  1.41 us

profile of v4, /device:TPU:1, one launch (start us, length us, event | category | flops | bytes accessed | tf_op | source)
XLA Modules:
  0.0 59.0 jit_solution(13727941380089150123)
XLA Ops:
  0.6 57.0 %projected_gram.1 = (f32[16,4096]{1,0:T(8,128)S(1)}, f32[16,4096]{1,0:T(8,128)S(1)}) custom-call(bf16[1728,2048]{1,0:T(8,128)(2,1)} %bitcast.1, bf16[2048,640]{1,0:T(8,128)(2,1)} %og.1, bf16[64,1728]{1,0:T(8,128)(2,1)} %pin_h.1, bf16[64,640]{1,0:T(8,128)(2,1)} %pout_h.1, s32[1,2048]{1,0:T(1,128)} %seg_h.1), custom_call_target="tpu_custom_call" | custom-call | tf_op jit(solution)/shard_map/projected_gram/pallas_call | solution.py:465
  57.6 0.7 %copy.9 = f32[16,4096]{1,0:T(8,128)} copy(f32[16,4096]{1,0:T(8,128)S(1)} %get-tuple-element.2) | data formatting | bytes 524288
  58.3 0.7 %copy.10 = f32[16,4096]{1,0:T(8,128)} copy(f32[16,4096]{1,0:T(8,128)S(1)} %get-tuple-element.3) | data formatting | bytes 524288

commit v5 on v4

--- a/solution.py
+++ b/solution.py
@@ -266,20 +266,16 @@
             out = moved if out is None else jnp.where(group == g, moved, out)
         return out
 
-    for cq in range(4):
-        for z in range(2):
-            for k in range(2):
-                gbuf2[cq, z, k] = regroup([nat[8 * k + 2 * g + z] for g in range(4)], cq)
-
     bs = []
-    for k in (2, 1, 3):
-        to = (c + k) % 4
-        cp = rc(gbuf2.at[to], brecv.at[k - 1], b_s.at[k - 1], b_r.at[k - 1], dp, to * 2 + h)
-        launch(cp)
-        bs.append(cp)
-    for cp in bs:
-        cp.wait_recv()
-    fown[...] = (gbuf2[c] + brecv[0] + brecv[1] + brecv[2]) * scale[None, None]
+    for b in range(2):
+        for cq in range(4):
+            for z in range(2):
+                gbuf2[cq, b, z] = regroup([nat[8 * b + 2 * g + z] for g in range(4)], cq)
+        for k in (2, 1, 3):
+            to = (c + k) % 4
+            n = b * 3 + k - 1
+            bs.append(rc(gbuf2.at[to, b], brecv.at[k - 1, b], b_s.at[n], b_r.at[n], dp, to * 2 + h))
+            launch(bs[-1])
 
     far = (2, 1, 3, 0)
     yy = p // 4
@@ -290,9 +286,10 @@
     def spot(first, second):
         return (first * (4 - 3 * h) + second * (1 + 3 * h)) * 2 + zl
 
-    def c2(k):
+    def c2(b, k):
         to = (m + k) % MP
-        return rc(fown.at[to % 2], fpar.at[m], c2_s.at[k], c2_r.at[k], dp, to)
+        n = b * MP + k
+        return rc(fown.at[to % 2, b], fpar.at[m, b], c2_s.at[n], c2_r.at[n], dp, to)
 
     def near(z, k):
         src = fown.at[zl] if z == 0 else cc.at[1 - zl, u, v]
@@ -323,32 +320,55 @@
             2 * c + th,
         )
 
-    for k in (4, 5, 3, 2, 6, 7, 1):
-        launch(c2(k))
+    def own(b):
+        for k in range(3):
+            bs[3 * b + k].wait_recv()
+        done = (gbuf2[c, b] + brecv[0, b] + brecv[1, b] + brecv[2, b]) * scale[None]
+        for z in range(2):
+            fown[z, b] = done[z]
+        for k in (4, 5, 3, 2, 6, 7, 1):
+            launch(c2(b, k))
+        fpar[m, b] = fown[h, b]
+        cc[zl, u, v, b] = fown[zl, b]
+
+    def rows(b):
+        for k in range(1, MP):
+            c2(b, k).wait_recv()
+        for q in (b, b + 2):
+            for g in range(4):
+                fnat[4 * q + g] = regroup([fpar[2 * cq + q // 2, b] for cq in range(4)], g)
+        odd = (yy + b) % 2
+        for dz in (1, 0):
+            for i in (1, 0):
+                for dx in far:
+                    k = (2 * i + odd) * 8 + dx * 2 + dz
+                    if i + dx + dz:
+                        c3(k).start()
+                    else:
+
+                        @pl.when(odd == 1)
+                        def _():
+                            c3(k).start()
+
+    own(0)
+    own(1)
     x1 = rc(fown.at[1 - zl], cc.at[zl, u, v], c1_s.at[0], c1_r.at[0], 2 * p + 1 - zl, m)
     launch(x1)
     for k in far[:3]:
         launch(near(0, k))
-    cc[zl, u, v] = fown[zl]
-    fpar[m] = fown[h]
     x1.wait_recv()
     for k in far[:3]:
         launch(near(1, k))
-    for z in range(2):
-        for k in far[:3]:
-            near(z, k).wait_recv()
-        for k in far[:3]:
-            launch(wide(z, k))
-    for k in range(1, MP):
-        c2(k).wait_recv()
-    for q in range(4):
-        for g in range(4):
-            fnat[4 * q + g] = regroup([fpar[2 * cq + q // 2, q % 2] for cq in range(4)], g)
-    for dz in (1, 0):
-        for dy in far:
-            for dx in far:
-                if dy + dx + dz:
-                    c3(dy * 8 + dx * 2 + dz).start()
+    for k in far[:3]:
+        near(0, k).wait_recv()
+    for k in far[:3]:
+        launch(wide(0, k))
+    rows(0)
+    for k in far[:3]:
+        near(1, k).wait_recv()
+    for k in far[:3]:
+        launch(wide(1, k))
+    rows(1)
     sent.append(lambda: each(DP, lambda k: c3(k).wait_send()))
     rr[zl, p] = fnat[p]
     ft = rc(fnat, fnatp, ft_s, ft_r, dp, partner)
@@ -447,12 +467,12 @@
         dma((6,)),
         dma,
         dma,
-        dma((3,)),
-        dma((3,)),
-        dma((32,)),
-        dma((32,)),
-        dma((8,)),
-        dma((8,)),
+        dma((6,)),
+        dma((6,)),
+        dma((16,)),
+        dma((16,)),
+        dma((16,)),
+        dma((16,)),
         dma((32,)),
         dma((32,)),
         dma((2,)),

time: 59.1 us -> 58.5 us (0.990)
  Pallas kernels: 57 us -> 56.4 us
    pallas_call x1, Pallas kernels: 57 us -> 56.4 us  [body(): pl.pallas_call(kernel, out_shape=(pltpu.VMEM((EX, 4096), F32), pltpu.VMEM...]
where the time goes in v5:
time: 58.5 us
  Pallas kernels  56.4 us (96%)
  local copies, waits for them, and re-layouts  1.41 us (2%)
  between operations  0.64 us (1%)
    pallas_call x1, Pallas kernels, body(): pl.pallas_call(kernel, out_shape=(pltpu.VMEM((EX, 4096), F32), pltpu.VMEM...  56.4 us
    unnamed x2, local copies, waits for them, and re-layouts  1.41 us

profile of v5, /device:TPU:1, one launch (start us, length us, event | category | flops | bytes accessed | tf_op | source)
XLA Modules:
  0.0 58.5 jit_solution(11048121211696539615)
XLA Ops:
  0.6 56.4 %projected_gram.1 = (f32[16,4096]{1,0:T(8,128)S(1)}, f32[16,4096]{1,0:T(8,128)S(1)}) custom-call(bf16[1728,2048]{1,0:T(8,128)(2,1)} %bitcast.1, bf16[2048,640]{1,0:T(8,128)(2,1)} %og.1, bf16[64,1728]{1,0:T(8,128)(2,1)} %pin_h.1, bf16[64,640]{1,0:T(8,128)(2,1)} %pout_h.1, s32[1,2048]{1,0:T(1,128)} %seg_h.1), custom_call_target="tpu_custom_call" | custom-call | tf_op jit(solution)/shard_map/projected_gram/pallas_call | solution.py:485
  57.0 0.7 %copy.9 = f32[16,4096]{1,0:T(8,128)} copy(f32[16,4096]{1,0:T(8,128)S(1)} %get-tuple-element.2) | data formatting | bytes 524288
  57.7 0.7 %copy.10 = f32[16,4096]{1,0:T(8,128)} copy(f32[16,4096]{1,0:T(8,128)S(1)} %get-tuple-element.3) | data formatting | bytes 524288

commit v6 on v5

--- a/solution.py
+++ b/solution.py
@@ -104,6 +104,9 @@
             device_id_type=MESH,
         )
 
+    barrier = pltpu.get_barrier_semaphore()
+    for k in range(1, MP):
+        pl.semaphore_signal(barrier, inc=1, device_id=(dp, (m + k) % MP), device_id_type=MESH)
     sent = []
 
     def drain():
@@ -114,12 +117,8 @@
         copy.start()
         sent.append(copy.wait_send)
 
-    def launch_each(n, f):
-        each(n, lambda k: f(k).start())
-        sent.append(lambda: each(n, lambda k: f(k).wait_send()))
-
-    def each(n, f):
-        lax.fori_loop(1, n, lambda k, v: (f(k), v)[1], 0)
+    def bytes_of(ref, sem):
+        return pltpu.make_async_copy(ref, ref, sem).wait
 
     owners = [(c + 2) % 4, (c + 1) % 4, (c + 3) % 4, c]
     blocks = []
@@ -139,19 +138,11 @@
         b.start()
         loads.append((a, b))
 
-    barrier = pltpu.get_barrier_semaphore()
-
     def greet_dp(k, carry):
         pl.semaphore_signal(barrier, inc=1, device_id=((dp + k) % DP, m), device_id_type=MESH)
         return carry
 
     lax.fori_loop(1, DP, greet_dp, 0)
-
-    def greet_own(k, carry):
-        pl.semaphore_signal(barrier, inc=1, device_id=(dp, (m + k) % MP), device_id_type=MESH)
-        return carry
-
-    lax.fori_loop(1, MP, greet_own, 0)
 
     def greet_plane(k, carry):
         pl.semaphore_signal(
@@ -266,16 +257,14 @@
             out = moved if out is None else jnp.where(group == g, moved, out)
         return out
 
-    bs = []
     for b in range(2):
         for cq in range(4):
             for z in range(2):
                 gbuf2[cq, b, z] = regroup([nat[8 * b + 2 * g + z] for g in range(4)], cq)
         for k in (2, 1, 3):
             to = (c + k) % 4
-            n = b * 3 + k - 1
-            bs.append(rc(gbuf2.at[to, b], brecv.at[k - 1, b], b_s.at[n], b_r.at[n], dp, to * 2 + h))
-            launch(bs[-1])
+            rc(gbuf2.at[to, b], brecv.at[k - 1, b], b_s.at[b], b_r.at[b], dp, to * 2 + h).start()
+        sent.append(bytes_of(brecv.at[:, b], b_s.at[b]))
 
     far = (2, 1, 3, 0)
     yy = p // 4
@@ -288,89 +277,85 @@
 
     def c2(b, k):
         to = (m + k) % MP
-        n = b * MP + k
-        return rc(fown.at[to % 2, b], fpar.at[m, b], c2_s.at[n], c2_r.at[n], dp, to)
+        return rc(fown.at[to % 2, b], fpar.at[m, b], c2_s.at[b], c2_r.at[b], dp, to)
 
     def near(z, k):
         src = fown.at[zl] if z == 0 else cc.at[1 - zl, u, v]
         dst = cc.at[(zl + z) % 2, u, v]
-        n = 1 + z * 6 + k
+        n = 1 + z
         return rc(src, dst, c1_s.at[n], c1_r.at[n], spot(u, (v + k) % 4), m)
 
     def wide(z, k):
         row = cc.at[(zl + z) % 2, u]
-        n = 4 + z * 6 + k
+        n = 3 + z
         return rc(row, row, c1_s.at[n], c1_r.at[n], spot((u + k) % 4, v), m)
 
-    def c3(k):
-        tp = (yy + k // 8) % 4 * 4 + (xx + k // 2 % 4) % 4
-        to = tp * 2 + (zl + k % 2) % 2
-        return rc(fnat.at[tp], rr.at[zl, p], c3_s.at[k], c3_r.at[k], to, m)
-
-    def dd(k):
-        ty = (yy + k // 8) % 4
-        tx = (xx + k // 2 % 4) % 4
-        th = (h + k % 2) % 2
-        return rc(
-            gb.at[ty, tx, th],
-            gg.at[2 * p + h],
-            dd_s.at[k],
-            dd_r.at[k],
-            (ty * 4 + tx) * 2 + zl,
-            2 * c + th,
-        )
+    xs = [(xx + k) % 4 for k in range(4)]
+    ys = [(yy + k) % 4 for k in range(4)]
+    zs = [zl, 1 - zl]
+    hs = [h, 1 - h]
+    mine = zl * XY + p
+
+    def c3(ty, tx, tz):
+        tp = ty * 4 + tx
+        return rc(fnat.at[tp], rr.at[mine], c3_s, c3_r, tp * 2 + tz, m)
+
+    def dd(ty, tx, th):
+        src = gb.at[ty, tx, th]
+        return rc(src, gg.at[2 * p + h], dd_s, dd_r, (ty * 4 + tx) * 2 + zl, 2 * c + th)
 
     def own(b):
-        for k in range(3):
-            bs[3 * b + k].wait_recv()
+        bytes_of(brecv.at[:, b], b_r.at[b])()
         done = (gbuf2[c, b] + brecv[0, b] + brecv[1, b] + brecv[2, b]) * scale[None]
         for z in range(2):
             fown[z, b] = done[z]
         for k in (4, 5, 3, 2, 6, 7, 1):
-            launch(c2(b, k))
+            c2(b, k).start()
+        sent.append(bytes_of(fpar.at[0:7, b], c2_s.at[b]))
         fpar[m, b] = fown[h, b]
         cc[zl, u, v, b] = fown[zl, b]
 
     def rows(b):
-        for k in range(1, MP):
-            c2(b, k).wait_recv()
+        bytes_of(fpar.at[0:7, b], c2_r.at[b])()
         for q in (b, b + 2):
             for g in range(4):
                 fnat[4 * q + g] = regroup([fpar[2 * cq + q // 2, b] for cq in range(4)], g)
         odd = (yy + b) % 2
         for dz in (1, 0):
             for i in (1, 0):
+                ty = (yy + 2 * i + odd) % 4
                 for dx in far:
-                    k = (2 * i + odd) * 8 + dx * 2 + dz
                     if i + dx + dz:
-                        c3(k).start()
+                        c3(ty, xs[dx], zs[dz]).start()
                     else:
 
                         @pl.when(odd == 1)
                         def _():
-                            c3(k).start()
+                            c3(ty, xs[dx], zs[dz]).start()
 
     own(0)
     own(1)
     x1 = rc(fown.at[1 - zl], cc.at[zl, u, v], c1_s.at[0], c1_r.at[0], 2 * p + 1 - zl, m)
     launch(x1)
-    for k in far[:3]:
-        launch(near(0, k))
+    few = cc.at[0, 0, 0:3]
+    many = cc.at[0, 0:3]
+
+    def three(f, z, ref, n):
+        for k in far[:3]:
+            f(z, k).start()
+        sent.append(bytes_of(ref, c1_s.at[n]))
+
+    three(near, 0, few, 1)
     x1.wait_recv()
-    for k in far[:3]:
-        launch(near(1, k))
-    for k in far[:3]:
-        near(0, k).wait_recv()
-    for k in far[:3]:
-        launch(wide(0, k))
+    three(near, 1, few, 2)
+    bytes_of(few, c1_r.at[1])()
+    three(wide, 0, many, 3)
     rows(0)
-    for k in far[:3]:
-        near(1, k).wait_recv()
-    for k in far[:3]:
-        launch(wide(1, k))
+    bytes_of(few, c1_r.at[2])()
+    three(wide, 1, many, 4)
     rows(1)
-    sent.append(lambda: each(DP, lambda k: c3(k).wait_send()))
-    rr[zl, p] = fnat[p]
+    sent.append(bytes_of(rr.at[0:31], c3_s))
+    rr[mine] = fnat[p]
     ft = rc(fnat, fnatp, ft_s, ft_r, dp, partner)
     launch(ft)
 
@@ -378,8 +363,7 @@
         return rc(cc.at[z], ccp.at[z], c4_s.at[z], c4_r.at[z], dp, partner)
 
     for z in range(2):
-        for k in far[:3]:
-            wide(z, k).wait_recv()
+        bytes_of(many, c1_r.at[3 + z])()
         launch(swap((zl + z) % 2))
     ft.wait_recv()
     for q in range(XY):
@@ -403,21 +387,21 @@
     swap(zl).wait_recv()
     swap(1 - zl).wait_recv()
     turned(ccp, 1 - h)
-    each(DP, lambda k: c3(k).wait_recv())
+    bytes_of(rr.at[0:31], c3_r)()
     rh, rl = split(rr[...].reshape(DP * EX, 128))
     right = jnp.concatenate([rh, rl], axis=1)
     for dy in far:
-        q = (yy + dy) % 4
+        q = ys[dy]
         both = dot(ath[q], right)
         res = both[:, 0:128] + both[:, 128:256] + dot(atl[q], rh)
         gb[q] = (res * (1.0 / (DP * EX))).reshape(4, 2, 16, 128)
         for dx in far:
             for dh in (1, 0):
                 if dy + dx + dh:
-                    dd(dy * 8 + dx * 2 + dh).start()
-    sent.append(lambda: each(DP, lambda k: dd(k).wait_send()))
+                    dd(q, xs[dx], hs[dh]).start()
+    sent.append(bytes_of(gg.at[0:31], dd_s))
     gg[2 * p + h] = gb[yy, xx, h]
-    each(DP, lambda k: dd(k).wait_recv())
+    bytes_of(gg.at[0:31], dd_r)()
     for i in range(DP):
         gram_o[:, i * 128 : i * 128 + 128] = gg[i]
 
@@ -455,7 +439,7 @@
         pltpu.VMEM((16, 16, 128), F32),
         pltpu.VMEM((2, 4, 4, 2, 16, 128), F32),
         pltpu.VMEM((2, 4, 4, 2, 16, 128), F32),
-        pltpu.VMEM((2, 16, 16, 128), F32),
+        pltpu.VMEM((32, 16, 128), F32),
         pltpu.VMEM((4, 128, 512), BF16),
         pltpu.VMEM((4, 128, 512), BF16),
         pltpu.VMEM((4, 4, 2, 16, 128), F32),
@@ -467,20 +451,20 @@
         dma((6,)),
         dma,
         dma,
-        dma((6,)),
-        dma((6,)),
-        dma((16,)),
-        dma((16,)),
-        dma((16,)),
-        dma((16,)),
-        dma((32,)),
-        dma((32,)),
-        dma((2,)),
-        dma((2,)),
-        dma,
-        dma,
-        dma((32,)),
-        dma((32,)),
+        dma((2,)),
+        dma((2,)),
+        dma((5,)),
+        dma((5,)),
+        dma((2,)),
+        dma((2,)),
+        dma,
+        dma,
+        dma((2,)),
+        dma((2,)),
+        dma,
+        dma,
+        dma,
+        dma,
     ]
     return pl.pallas_call(
         kernel,

time: 58.5 us -> 55.9 us (0.956)
  Pallas kernels: 56.4 us -> 53.8 us
    pallas_call x1, Pallas kernels: 56.4 us -> 53.8 us  [body(): pl.pallas_call(kernel, out_shape=(pltpu.VMEM((EX, 4096), F32), pltpu.VMEM...]
where the time goes in v6:
time: 55.9 us; the launch traced here: 55.8 us
  Pallas kernels  53.8 us (96%)
  local copies, waits for them, and re-layouts  1.41 us (3%)
  between operations  0.64 us (1%)
    pallas_call x1, Pallas kernels, body(): pl.pallas_call(kernel, out_shape=(pltpu.VMEM((EX, 4096), F32), pltpu.VMEM...  53.8 us
    unnamed x2, local copies, waits for them, and re-layouts  1.41 us

profile of v6, /device:TPU:1, one launch (start us, length us, event | category | flops | bytes accessed | tf_op | source)
XLA Modules:
  0.0 55.8 jit_solution(1797299165389785972)
XLA Ops:
  0.6 53.8 %projected_gram.1 = (f32[16,4096]{1,0:T(8,128)S(1)}, f32[16,4096]{1,0:T(8,128)S(1)}) custom-call(bf16[1728,2048]{1,0:T(8,128)(2,1)} %bitcast.1, bf16[2048,640]{1,0:T(8,128)(2,1)} %og.1, bf16[64,1728]{1,0:T(8,128)(2,1)} %pin_h.1, bf16[64,640]{1,0:T(8,128)(2,1)} %pout_h.1, s32[1,2048]{1,0:T(1,128)} %seg_h.1), custom_call_target="tpu_custom_call" | custom-call | tf_op jit(solution)/shard_map/projected_gram/pallas_call | solution.py:469
  54.4 0.7 %copy.9 = f32[16,4096]{1,0:T(8,128)} copy(f32[16,4096]{1,0:T(8,128)S(1)} %get-tuple-element.2) | data formatting | bytes 524288
  55.1 0.7 %copy.10 = f32[16,4096]{1,0:T(8,128)} copy(f32[16,4096]{1,0:T(8,128)S(1)} %get-tuple-element.3) | data formatting | bytes 524288

commit v7 on v6

--- a/solution.py
+++ b/solution.py
@@ -211,15 +211,14 @@
     zrel[1] = zrecv[1] + pmine[1, 64:128]
     zsend.append(zcopy(5, zrel.at[1], up))
     launch(zsend[5])
-    zsend[2].wait_recv()
-    zsend[3].wait_recv()
-    zsend[4].wait_recv()
-    zsend[5].wait_recv()
-    pown[0:64] = pmine[3, 0:64] + zrecv[2] + zrecv[4]
-    pown[64:128] = pmine[3, 64:128] + zrecv[3] + zrecv[5]
-
-    px = rc(pown, ppart, px_s, px_r, dp, partner)
-    launch(px)
+    px = []
+    for half, (direct, relayed) in enumerate(((2, 4), (3, 5))):
+        part = slice(64 * half, 64 * half + 64)
+        zsend[direct].wait_recv()
+        zsend[relayed].wait_recv()
+        pown[part] = pmine[3, part] + zrecv[direct] + zrecv[relayed]
+        px.append(rc(pown.at[part], ppart.at[part], px_s.at[half], px_r.at[half], dp, partner))
+        launch(px[half])
 
     def weigh(s, toks, blk):
         ih, il = split(toks[0:64])
@@ -245,7 +244,8 @@
 
     weigh(0, pown, m)
     g0 = grads(0)
-    px.wait_recv()
+    px[0].wait_recv()
+    px[1].wait_recv()
     weigh(1, ppart, partner)
     nat = (g0 + grads(1)).reshape(16, EX, 128)
     group = lax.broadcasted_iota(jnp.int32, (EX, 128), 1) // 32
@@ -406,6 +406,17 @@
         gram_o[:, i * 128 : i * 128 + 128] = gg[i]
 
     drain()
+
+
+def store(feat, gram, feat_o, gram_o, sem):
+    copies = [
+        pltpu.make_async_copy(feat, feat_o, sem.at[0]),
+        pltpu.make_async_copy(gram, gram_o, sem.at[1]),
+    ]
+    for copy in copies:
+        copy.start()
+    for copy in copies:
+        copy.wait()
 
 
 def body(hidden, out_grad, proj_in, proj_out, segment_ids):
@@ -449,8 +460,8 @@
         dma((4,)),
         dma((6,)),
         dma((6,)),
-        dma,
-        dma,
+        dma((2,)),
+        dma((2,)),
         dma((2,)),
         dma((2,)),
         dma((5,)),
@@ -466,7 +477,7 @@
         dma,
         dma,
     ]
-    return pl.pallas_call(
+    results = pl.pallas_call(
         kernel,
         out_shape=(
             pltpu.VMEM((EX, 4096), F32),
@@ -480,6 +491,18 @@
         ),
         name="projected_gram",
     )(hidden, out_grad, proj_in, proj_out, segment_ids)
+    return pl.pallas_call(
+        store,
+        out_shape=(
+            jax.ShapeDtypeStruct((EX, 4096), F32),
+            jax.ShapeDtypeStruct((16, 4096), F32),
+        ),
+        in_specs=[vmem, vmem],
+        out_specs=(hbm, hbm),
+        scratch_shapes=[dma((2,))],
+        compiler_params=pltpu.CompilerParams(vmem_limit_bytes=1 << 20),
+        name="store_results",
+    )(*results)
 
 
 def solution(mesh):

time: 55.9 us -> 55.3 us (0.989)
  local copies, waits for them, and re-layouts: 1.41 us -> 0 us
  Pallas kernels: 53.8 us -> 54.6 us
    unnamed x2 -> x0, local copies, waits for them, and re-layouts: 1.41 us -> none
    pallas_call x0 -> x1, Pallas kernels: none -> 0.81 us  [body(): pl.pallas_call(store, out_shape=(jax.ShapeDtypeStruct((EX, 4096), F32), j...]
where the time goes in v7:
time: 55.3 us; the launch traced here: 55.2 us
  Pallas kernels  54.6 us (99%)
  between operations  0.64 us (1%)
    pallas_call x1, Pallas kernels, body(): pl.pallas_call(kernel, out_shape=(pltpu.VMEM((EX, 4096), F32), pltpu.VMEM...  53.8 us

profile of v7, /device:TPU:1, one launch (start us, length us, event | category | flops | bytes accessed | tf_op | source)
XLA Modules:
  0.0 55.2 jit_solution(1148327898579278796)
XLA Ops:
  0.6 53.8 %projected_gram.1 = (f32[16,4096]{1,0:T(8,128)S(1)}, f32[16,4096]{1,0:T(8,128)S(1)}) custom-call(bf16[1728,2048]{1,0:T(8,128)(2,1)} %bitcast.1, bf16[2048,640]{1,0:T(8,128)(2,1)} %og.1, bf16[64,1728]{1,0:T(8,128)(2,1)} %pin_h.1, bf16[64,640]{1,0:T(8,128)(2,1)} %pout_h.1, s32[1,2048]{1,0:T(1,128)} %seg_h.1), custom_call_target="tpu_custom_call" | custom-call | tf_op jit(solution)/shard_map/projected_gram/pallas_call | solution.py:480
  54.4 0.8 %store_results.1 = (f32[16,4096]{1,0:T(8,128)}, f32[16,4096]{1,0:T(8,128)}) custom-call(f32[16,4096]{1,0:T(8,128)S(1)} %get-tuple-element.4.feat, f32[16,4096]{1,0:T(8,128)S(1)} %get-tuple-element.5.gram), custom_call_target="tpu_custom_call" | custom-call | tf_op jit(solution)/shard_map/store_results/pallas_call | solution.py:494
